TPU v7x, 32 devices: a whole 2x2x4 slice. The times are simulated.
32 devices in a mesh: dp: 2 (over x), t: 4 (over z), stage: 4 (over y, core).
Axes of the slice: x: 2, y: 2, z: 4, core: 2. Of those that a mesh axis runs over, the one named last changes fastest.
Arguments:
- hidden: bfloat16 [8, 8, 1536, 2048], P(('dp', 'stage')), parts along dimension 0
- w_query: bfloat16 [2048, 3072], P(None, 't')
- w_dkv: bfloat16 [2048, 576], replicated
- latent_gain: bfloat16 [512], replicated
- w_uk: bfloat16 [512, 2048], P(None, 't')
- w_uv: bfloat16 [512, 2048], P(None, 't')
- w_out: bfloat16 [2048, 2048], P('t')
Outputs:
- output 1: bfloat16 [8, 8, 1536, 2048], P(('dp', 'stage')), parts along dimension 0
- output 2: bfloat16 [8, 8, 1536, 576], P(('dp', 'stage'), 't'), parts along dimension 0
There are 2 independent parts. A program takes and returns all parts, laid end to end along the dimension named above; an argument that names none is the same for every part.
All inputs are finite; a program needn't handle non-finite values.
Results may differ from a plain program's by a relative error of at most 0.0108288.
Values are sent between devices in bfloat16 or wider.
A program may use at most 1 GiB of HBM per device.

v0:
```python
import jax
import jax.numpy as jnp
from jax import lax
from jax.sharding import PartitionSpec as P

NOPE_DIM = 128
ROPE_DIM = 64
V_DIM = 128
NORM_EPS = 1e-6
ROPE_BASE = 10000.0


def rope_tables(seq_len):
    half_dim = ROPE_DIM // 2
    positions = jnp.arange(seq_len, dtype=jnp.float32)
    inv_freq = ROPE_BASE ** (-jnp.arange(half_dim, dtype=jnp.float32) / half_dim)
    angles = positions[:, None] * inv_freq[None, :]
    return jnp.cos(angles), jnp.sin(angles)


def apply_rope(vecs, cos_tab, sin_tab):
    half_dim = vecs.shape[-1] // 2
    as_f32 = vecs.astype(jnp.float32)
    low_half = as_f32[..., :half_dim]
    high_half = as_f32[..., half_dim:]
    rotated = jnp.concatenate([low_half * cos_tab - high_half * sin_tab, high_half * cos_tab + low_half * sin_tab], axis=-1)
    return rotated.astype(jnp.bfloat16)


def latent_rows(tokens, w_dkv, latent_gain, cos_tab, sin_tab):
    kv_rank = latent_gain.shape[0]
    compressed = jnp.einsum("bsd,dc->bsc", tokens, w_dkv, preferred_element_type=jnp.float32).astype(jnp.bfloat16)
    c_raw = compressed[..., :kv_rank].astype(jnp.float32)
    inv_rms = lax.rsqrt(jnp.mean(c_raw * c_raw, axis=-1, keepdims=True) + NORM_EPS)
    c_kv = (c_raw * inv_rms * latent_gain.astype(jnp.float32)).astype(jnp.bfloat16)
    k_rope = apply_rope(compressed[..., kv_rank:], cos_tab, sin_tab)
    return jnp.concatenate([c_kv, k_rope], axis=-1)


def causal_heads(q_nope, q_rope, k_nope, k_rope, values):
    seq_len = q_nope.shape[1]
    n_blocks = max(1, min(8, seq_len // 128))
    block_len = seq_len // n_blocks
    score_scale = (q_nope.shape[-1] + q_rope.shape[-1]) ** -0.5
    pieces = []
    for block_idx in range(n_blocks):
        start_row = block_idx * block_len
        stop_row = start_row + block_len
        scores = jnp.einsum("bqhe,bkhe->bhqk", q_nope[:, start_row:stop_row], k_nope[:, :stop_row], preferred_element_type=jnp.float32)
        scores = scores + jnp.einsum("bqhe,bke->bhqk", q_rope[:, start_row:stop_row], k_rope[:, :stop_row], preferred_element_type=jnp.float32)
        q_pos = start_row + jnp.arange(block_len)[:, None]
        k_pos = jnp.arange(stop_row)[None, :]
        scores = jnp.where(k_pos <= q_pos, scores * score_scale, -jnp.inf)
        row_peak = jnp.max(scores, axis=-1, keepdims=True)
        weights = jnp.exp(scores - row_peak)
        row_total = jnp.sum(weights, axis=-1)
        mixed = jnp.einsum("bhqk,bkhe->bqhe", weights.astype(jnp.bfloat16), values[:, :stop_row], preferred_element_type=jnp.float32)
        pieces.append((mixed / jnp.transpose(row_total, (0, 2, 1))[..., None]).astype(jnp.bfloat16))
    return jnp.concatenate(pieces, axis=1)


def attention_partial(tokens, latent, w_query, w_uk, w_uv, w_out, cos_tab, sin_tab):
    kv_rank = w_uk.shape[0]
    batch, seq_len = tokens.shape[0], tokens.shape[1]
    heads_here = w_uk.shape[1] // NOPE_DIM
    queries = jnp.einsum("bsd,dn->bsn", tokens, w_query, preferred_element_type=jnp.float32).astype(jnp.bfloat16)
    queries = queries.reshape(batch, seq_len, heads_here, NOPE_DIM + ROPE_DIM)
    q_rope = apply_rope(queries[..., NOPE_DIM:], cos_tab[:, None, :], sin_tab[:, None, :])
    k_nope = jnp.einsum("bsr,rn->bsn", latent[..., :kv_rank], w_uk, preferred_element_type=jnp.float32).astype(jnp.bfloat16)
    k_nope = k_nope.reshape(batch, seq_len, heads_here, NOPE_DIM)
    values = jnp.einsum("bsr,rn->bsn", latent[..., :kv_rank], w_uv, preferred_element_type=jnp.float32).astype(jnp.bfloat16)
    values = values.reshape(batch, seq_len, heads_here, V_DIM)
    head_mix = causal_heads(queries[..., :NOPE_DIM], q_rope, k_nope, latent[..., kv_rank:], values)
    head_mix = head_mix.reshape(batch, seq_len, heads_here * V_DIM)
    return jnp.einsum("bsn,nd->bsd", head_mix, w_out, preferred_element_type=jnp.float32)


def solution(mesh):
    n_tp = mesh.shape["t"]
    half_stage = mesh.shape["stage"] // 2
    hand_pairs = [(source_idx, source_idx + half_stage) for source_idx in range(half_stage)]
    slot_spec = P(("dp", "stage"), None, None, None)
    cache_spec = P(("dp", "stage"), "t", None, None)

    def device_step(hidden, w_query, w_dkv, latent_gain, w_uk, w_uv, w_out):
        tokens = hidden[0]
        local_rows = tokens.shape[0] // n_tp
        t_index = lax.axis_index("t")
        cos_tab, sin_tab = rope_tables(tokens.shape[1])
        my_tokens = lax.dynamic_slice_in_dim(tokens, t_index * local_rows, local_rows, axis=0)
        my_latent = latent_rows(my_tokens, w_dkv, latent_gain, cos_tab, sin_tab)
        all_latent = lax.all_gather(my_latent, "t", axis=0, tiled=True)
        handed = lax.ppermute(my_latent, "stage", hand_pairs)
        part_sum = attention_partial(tokens, all_latent, w_query, w_uk, w_uv, w_out, cos_tab, sin_tab)
        summed = lax.psum(part_sum.astype(jnp.bfloat16), "t")
        is_prompt = lax.axis_index("stage") < half_stage
        out_rows = jnp.where(is_prompt, summed, jnp.zeros_like(summed))
        return out_rows[None], handed[None]

    return jax.shard_map(device_step, mesh=mesh, in_specs=(slot_spec, P(None, "t"), P(None, None), P(None), P(None, "t"), P(None, "t"), P("t", None)), out_specs=(slot_spec, cache_spec), check_vma=False)
```

profile of v0, /device:TPU:0, one launch (start us, length us, event | category | flops | bytes accessed | tf_op | source)
XLA Modules:
  0.0 2448.1 jit_solution(12126264347729076433)
XLA Ops:
  7.3 11.4 fusion.77
  29.9 46.0 %fusion.35 = bf16[8,1536,768]{1,2,0:T(8,128)(2,1)} fusion(bf16[1,8,1536,2048]{3,2,1,0:T(8,128)(2,1)} %param.7, bf16[2048,768]{1,0:T(8,128)(2,1)S(1)} %copy-done), kind=kOutput, calls=%fused_computation.46 | convolution fusion | flops 38664142848 | bytes 72351744 | tf_op jit(solution)/shard_map/bsd,dn->bsn/dot_general | solution.py:66
  83.8 186.8 %all-gather.2.cloned.1.call-done = bf16[8,1536,576]{1,2,0:T(8,128)(2,1)} async-done(((bf16[2,1536,576]{1,2,0:T(8,128)(2,1)}), bf16[8,1536,576]{1,2,0:T(8,128)(2,1)}) %all-gather.2.cloned.1.call-update) | async-done | bytes 14155792 | tf_op jit(solution)/shard_map/all_gather | solution.py:92
  270.7 13.1 convolution_convert_fusion.1
  289.7 8.6 fusion.83
  298.3 16.6 fusion.56
  323.1 15.0 convolution_convert_fusion.2
  366.3 17.5 fusion.207
  391.2 9.9 fusion.157
  401.1 9.5 fusion.185
  410.6 15.8 fusion.208
  434.7 11.2 fusion.162
  445.9 17.1 fusion.209
  463.0 9.3 fusion.16
  472.3 14.2 fusion.147
  486.5 15.5 fusion.170
  502.0 25.7 %fusion.210 = (f32[8,4,192]{2,1,0:T(4,128)S(1)}, f32[8,4,192,1152]{3,2,1,0:T(8,128)}) fusion(f32[8,1152,192,4]{1,2,3,0:T(8,128)} %fusion.170, bf16[8,1536,4,128]{1,3,2,0:T(8,128)(2,1)} %bitcast.190, bf16[8,1536,4,192]{1,3,2,0:T(8,128)(2,1)} %bitcast.199, pred[192,1152]{1,0:T(8,128)(4,1)S(1)} %copy-done.7), kind=kOutput, calls=%fused_computation.213 | convolution fusion | flops 1840244736 | bytes 68403200 | tf_op jit(solution)/shard_map/bqhe,bkhe->bhqk/dot_general | solution.py:49
  527.7 10.0 fusion.14
  537.7 15.7 fusion.142
  553.4 15.9 fusion.169
  569.3 28.5 %fusion.211 = (f32[8,4,192]{2,1,0:T(4,128)S(1)}, f32[8,4,192,1344]{3,2,1,0:T(8,128)}) fusion(f32[8,1344,192,4]{1,2,3,0:T(8,128)} %fusion.169, bf16[8,1536,4,128]{1,3,2,0:T(8,128)(2,1)} %bitcast.191, bf16[8,1536,4,192]{1,3,2,0:T(8,128)(2,1)} %bitcast.200, pred[192,1344]{1,0:T(8,128)(4,1)S(1)} %copy-done.6), kind=kOutput, calls=%fused_computation.214 | convolution fusion | flops 2146953216 | bytes 81547264 | tf_op jit(solution)/shard_map/bqhe,bkhe->bhqk/dot_general | solution.py:49
  597.9 13.9 fusion.8
  611.7 18.4 fusion.134
  630.1 17.5 fusion.168
  647.6 29.3 %fusion.212 = (f32[8,4,192]{2,1,0:T(4,128)S(1)}, f32[8,4,192,1536]{3,2,1,0:T(8,128)}) fusion(f32[8,1536,192,4]{1,2,3,0:T(8,128)} %fusion.168, bf16[8,1536,4,128]{1,3,2,0:T(8,128)(2,1)} %bitcast.192, bf16[8,1536,4,192]{1,3,2,0:T(8,128)(2,1)} %bitcast.201, pred[192,1536]{1,0:T(8,128)(4,1)S(1)} %copy-done.5), kind=kOutput, calls=%fused_computation.215 | convolution fusion | flops 2453661696 | bytes 90497024 | tf_op jit(solution)/shard_map/bqhe,bkhe->bhqk/dot_general | solution.py:49
  676.9 14.6 fusion.6
  691.6 19.3 fusion.139
  710.9 16.8 copy.100
  727.6 35.8 %convolution_convert_fusion = bf16[8,1536,2048]{2,1,0:T(8,128)(2,1)} fusion(bf16[8,1536,512]{1,2,0:T(8,128)(2,1)} %bitcast.202, bf16[512,2048]{1,0:T(8,128)(2,1)S(1)} %copy-done.14), kind=kOutput, calls=%fused_computation.3 | convolution fusion | flops 25794969600 | bytes 65011712 | tf_op jit(solution)/shard_map/bsn,nd->bsd/dot_general | solution.py:75
  768.6 74.3 %collective-permute-done = bf16[2,1536,576]{1,2,0:T(8,128)(2,1)} collective-permute-done((bf16[2,1536,576]{1,2,0:T(8,128)(2,1)}, bf16[2,1536,576]{1,2,0:T(8,128)(2,1)}, u32[]{:S(2)}, u32[]{:S(2)}) %collective-permute-start) | collective-permute-done | bytes 3538976 | tf_op jit(solution)/shard_map/ppermute | solution.py:93
  842.9 1560.3 %all-reduce.2.cloned.1.call-done = bf16[8,1536,2048]{2,1,0:T(8,128)(2,1)} async-done(((bf16[8,1536,2048]{2,1,0:T(8,128)(2,1)}), bf16[8,1536,2048]{2,1,0:T(8,128)(2,1)}) %all-reduce.2.cloned.1.call-update) | async-done | bytes 50331664 | tf_op jit(solution)/shard_map/psum | solution.py:95
  2403.1 33.6 %select_bitcast_fusion = bf16[1,8,1536,2048]{3,2,1,0:T(8,128)(2,1)} fusion(bf16[8,1536,2048]{2,1,0:T(8,128)(2,1)} %all-reduce.2.cloned.1.call-done, pred[]{:T(512)S(6)} %lt.6), kind=kLoop, calls=%fused_computation.2 | loop fusion | flops 25165824 | bytes 100663296 | tf_op jit(solution)/shard_map/broadcast_in_dim | solution.py:98
  (74 shorter events, 86.4 us)
Async XLA Ops:
  7.2 22.7 copy-start
  7.2 263.5 %all-gather.2.cloned.1.call-start = ((), (), s32[]{:S(2)}) async-start(), calls=%async_computation | async-start | bytes 17694720 | tf_op jit(solution)/shard_map/all_gather | solution.py:92
  7.2 12.9 copy-start.13
  23.2 2380.0 %all-reduce.2.cloned.1.call-start = ((), (), s32[]{:S(2)}) async-start(), calls=%async_computation.1 | async-start | bytes 100663296 | tf_op jit(solution)/shard_map/psum | solution.py:95
  298.3 16.6 copy-start.2
  298.3 16.6 copy-start.12
  314.9 8.2 copy-start.15
  319.3 2.6 copy-start.4
  338.1 6.9 copy-start.11
  358.2 8.0 copy-start.10
  391.2 9.9 copy-start.3
  401.1 9.5 copy-start.8
  434.7 11.2 copy-start.9
  486.5 15.5 copy-start.7
  553.4 15.9 copy-start.6
  630.1 17.5 copy-start.5
  710.9 16.8 copy-start.14
  763.5 79.4 %collective-permute-start = (bf16[2,1536,576]{1,2,0:T(8,128)(2,1)}, bf16[2,1536,576]{1,2,0:T(8,128)(2,1)}, u32[]{:S(2)}, u32[]{:S(2)}) collective-permute-start(bf16[2,1536,576]{1,2,0:T(8,128)(2,1)} %pad_maximum_fusion), channel_id=1, source_target_pairs={{0,2},{1,3},{4,6},{5,7},{8,10},{9,11},{12,14},{13,15},{16,18},{17,... | collective-permute-start | bytes 10616840 | tf_op jit(solution)/shard_map/ppermute | solution.py:93
  2403.1 37.6 %copy-start.1 = (bf16[2048,768]{1,0:T(8,128)(2,1)S(1)}, bf16[2048,768]{1,0:T(8,128)(2,1)}, u32[]{:S(2)}) copy-start(bf16[2048,768]{1,0:T(8,128)(2,1)} %param.8) | copy-start | bytes 9437188
Sparse Core Ops, SparseCore 0:
  23.3 247.3 all-gather.1
  763.6 1639.5 all-reduce.1
where the time goes:
time: 2450 us
  waiting for transfers between devices  1820 us (74%)
  matrix products  463 us (19%)
  other arithmetic  120 us (5%)
    psum x1, waiting for transfers between devices, device_step(): summed = lax.psum(part_sum.astype(jnp.bfloat16), 't')  1560 us
    all_gather x1, waiting for transfers between devices, device_step(): all_latent = lax.all_gather(my_latent, 't', axis=0, tiled=True)  187 us
    dot_general x8, matrix products, causal_heads(): jnp.einsum('bqhe,bkhe->bhqk', q_nope[:, start_row:stop_row], k_nope[:, :s...  148 us
    dot_general x8, matrix products, causal_heads(): jnp.einsum('bhqk,bkhe->bqhe', weights.astype(jnp.bfloat16), values[:, :st...  101 us
    dot_general x8, matrix products, causal_heads(): jnp.einsum('bqhe,bke->bhqk', q_rope[:, start_row:stop_row], k_rope[:, :st...  93.5 us
    ppermute x1, waiting for transfers between devices, device_step(): handed = lax.ppermute(my_latent, 'stage', hand_pairs)  74.3 us
    reduce_sum x8, other arithmetic, causal_heads(): row_total = jnp.sum(weights, axis=-1)  67.3 us
  transfers between devices with their start and end apart: 3, of which 3 were waited for; matrix products, arithmetic and copies ran while one was open for 2% of the time, Pallas kernels for 0%

commit v1 on v0

v1 whole, which is shorter than its diff:
```python
import functools

import jax
import jax.numpy as jnp
from jax import lax
from jax.experimental import pallas as pl
from jax.experimental.pallas import tpu as pltpu
from jax.sharding import PartitionSpec as P


NOPE_DIM = 128
ROPE_DIM = 64
V_DIM = 128
HEAD_DIM = NOPE_DIM + ROPE_DIM
NORM_EPS = 1e-6
ROPE_BASE = 10000.0
LOG2E = 1.4426950408889634
ROWS = 512
Q_ROWS = 256


def rope_tables(seq_len):
    half_dim = ROPE_DIM // 2
    positions = jnp.arange(seq_len, dtype=jnp.float32)
    inv_freq = ROPE_BASE ** (-jnp.arange(half_dim, dtype=jnp.float32) / half_dim)
    angles = positions[:, None] * inv_freq[None, :]
    return jnp.cos(angles), jnp.sin(angles)


def swap_halves(w, is_low):
    return jnp.where(is_low, pltpu.roll(w, 96, 1), pltpu.roll(w, 32, 1))


def latent_kernel(kv_rank, merged, *refs):
    if merged:
        meta, x_ref, in_ref, wd_ref, gain_ref, cos_ref, sin_ref, xin_ref, ckv_ref, krp_ref = refs
    else:
        meta, x_ref, wd_ref, gain_ref, cos_ref, sin_ref, ckv_ref, krp_ref = refs
    f32 = jnp.float32

    def body():
        x = x_ref[0]
        if merged:
            x = jnp.where(meta[1] == 1, x, in_ref[0])
            xin_ref[0] = x
        comp = jnp.dot(x, wd_ref[...], preferred_element_type=f32).astype(jnp.bfloat16)
        raw = comp[:, :kv_rank].astype(f32)
        inv_rms = lax.rsqrt(jnp.mean(raw * raw, axis=-1, keepdims=True) + NORM_EPS)
        ckv_ref[0] = (raw * inv_rms * gain_ref[...]).astype(jnp.bfloat16)
        w = comp[:, kv_rank:].astype(f32)
        lane = lax.broadcasted_iota(jnp.int32, w.shape, 1)
        is_low = (lane % ROPE_DIM) < ROPE_DIM // 2
        roped = w * cos_ref[...] + swap_halves(w, is_low) * sin_ref[...]
        krp_ref[0, :, :128] = roped.astype(jnp.bfloat16)
        krp_ref[0, :, 128:] = pltpu.roll(roped, 64, 1).astype(jnp.bfloat16)

    pl.when(meta[0] == 1)(body)


def latent_call(meta, n_req, tokens, arrived, w_dkv, gain, cos, sin):
    _, seq_len, d_model = tokens.shape
    kv_rank = gain.shape[-1]
    in_specs = [pl.BlockSpec((1, ROWS, d_model), lambda r, i, m: (m[2 + r], i, 0))]
    operands = [meta, tokens]
    out_shape = [
        jax.ShapeDtypeStruct((n_req, seq_len, kv_rank), jnp.bfloat16),
        jax.ShapeDtypeStruct((n_req, seq_len, 256), jnp.bfloat16),
    ]
    out_specs = [
        pl.BlockSpec((1, ROWS, kv_rank), lambda r, i, m: (r, i, 0)),
        pl.BlockSpec((1, ROWS, 256), lambda r, i, m: (r, i, 0)),
    ]
    if arrived is not None:
        in_specs.append(pl.BlockSpec((1, ROWS, d_model), lambda r, i, m: (r, i, 0)))
        operands.append(arrived)
        out_shape.insert(0, jax.ShapeDtypeStruct((n_req, seq_len, d_model), jnp.bfloat16))
        out_specs.insert(0, pl.BlockSpec((1, ROWS, d_model), lambda r, i, m: (r, i, 0)))
    in_specs += [
        pl.BlockSpec(w_dkv.shape, lambda r, i, m: (0, 0)),
        pl.BlockSpec((1, kv_rank), lambda r, i, m: (0, 0)),
        pl.BlockSpec((ROWS, 128), lambda r, i, m: (i, 0)),
        pl.BlockSpec((ROWS, 128), lambda r, i, m: (i, 0)),
    ]
    return pl.pallas_call(
        functools.partial(latent_kernel, kv_rank, arrived is not None),
        out_shape=out_shape,
        grid_spec=pltpu.PrefetchScalarGridSpec(num_scalar_prefetch=1, grid=(n_req, seq_len // ROWS), in_specs=in_specs, out_specs=out_specs),
        compiler_params=pltpu.CompilerParams(vmem_limit_bytes=48 * 1024 * 1024),
        cost_estimate=pl.CostEstimate(flops=2 * n_req * seq_len * d_model * w_dkv.shape[1], bytes_accessed=n_req * seq_len * d_model * 2, transcendentals=0),
    )(*operands, w_dkv, gain, cos, sin)


def out_kernel(n_cols, *refs):
    meta, o_ref, w_ref = refs[:3]
    y_ref = refs[-1]

    def multiply(n, carry):
        cols = pl.ds(pl.multiple_of(n * ROWS, ROWS), ROWS)
        y_ref[0, :, cols] = jnp.dot(o_ref[0], w_ref[:, cols], preferred_element_type=jnp.float32).astype(jnp.bfloat16)
        return carry

    @pl.when(meta[0] == 1)
    def _():
        lax.fori_loop(0, n_cols // ROWS, multiply, 0)

    @pl.when(meta[0] != 1)
    def _():
        y_ref[...] = jnp.zeros_like(y_ref)


def out_call(meta, n_req, first_req, o_mix, w_out, into):
    _, seq_len, depth = o_mix.shape
    d_model = w_out.shape[1]
    block = (1, ROWS, d_model)
    in_specs = [pl.BlockSpec((1, ROWS, depth), lambda r, i, m: (r + first_req, i, 0)), pl.BlockSpec(w_out.shape, lambda r, i, m: (0, 0))]
    operands = [meta, o_mix, w_out]
    aliases = {}
    out_shape = jax.ShapeDtypeStruct((n_req, seq_len, d_model), jnp.bfloat16)
    if into is not None:
        in_specs.append(pl.BlockSpec(memory_space=pl.ANY))
        operands.append(into)
        aliases = {3: 0}
        out_shape = jax.ShapeDtypeStruct(into.shape, jnp.bfloat16)
    return pl.pallas_call(
        functools.partial(out_kernel, d_model),
        out_shape=out_shape,
        grid_spec=pltpu.PrefetchScalarGridSpec(num_scalar_prefetch=1, grid=(n_req, seq_len // ROWS), in_specs=in_specs, out_specs=pl.BlockSpec(block, lambda r, i, m: (m[1 + r], i, 0))),
        input_output_aliases=aliases,
        compiler_params=pltpu.CompilerParams(vmem_limit_bytes=48 * 1024 * 1024),
        cost_estimate=pl.CostEstimate(flops=2 * n_req * seq_len * depth * d_model, bytes_accessed=n_req * seq_len * d_model * 4, transcendentals=0),
    )(*operands)


def heads_kernel(n_heads, seq_len, chained, *refs):
    if chained:
        meta, x_ref, ckv_ref, krp_ref, wq_ref, wukv_ref, cos_ref, sin_ref, _, o_ref, q_s, k_s, v_s = refs
    else:
        meta, x_ref, ckv_ref, krp_ref, wq_ref, wukv_ref, cos_ref, sin_ref, o_ref, q_s, k_s, v_s = refs
    nope_cols = n_heads * NOPE_DIM
    f32 = jnp.float32

    def project(block_idx, carry):
        rows = pl.ds(pl.multiple_of(block_idx * ROWS, ROWS), ROWS)
        lat = ckv_ref[0, rows, :]
        k_nope = jnp.dot(lat, wukv_ref[0, :, :nope_cols], preferred_element_type=f32).astype(jnp.bfloat16)
        v_s[rows, :] = jnp.dot(lat, wukv_ref[0, :, nope_cols:], preferred_element_type=f32).astype(jnp.bfloat16)
        x = x_ref[0, rows, :]
        q_nope = jnp.dot(x, wq_ref[0, :, :nope_cols], preferred_element_type=f32).astype(jnp.bfloat16)
        q_rope = jnp.dot(x, wq_ref[0, :, nope_cols:], preferred_element_type=f32).astype(jnp.bfloat16)
        cos, sin = cos_ref[rows, :], sin_ref[rows, :]
        lane = lax.broadcasted_iota(jnp.int32, (ROWS, 128), 1)
        is_low = (lane % ROPE_DIM) < ROPE_DIM // 2
        for h in range(n_heads):
            if h % 2 == 0:
                w = q_rope[:, h * ROPE_DIM : h * ROPE_DIM + 128].astype(f32)
                roped = (w * cos + swap_halves(w, is_low) * sin).astype(jnp.bfloat16)
            q_s[h, rows, :NOPE_DIM] = q_nope[:, h * NOPE_DIM : (h + 1) * NOPE_DIM]
            q_s[h, rows, NOPE_DIM:] = roped
            k_s[h, rows, :NOPE_DIM] = k_nope[:, h * NOPE_DIM : (h + 1) * NOPE_DIM]
            k_s[h, rows, NOPE_DIM:] = krp_ref[0, rows, (h % 2) * 128 : (h % 2 + 1) * 128]
        return carry

    exponent_scale = HEAD_DIM ** -0.5 * LOG2E
    row = lax.broadcasted_iota(jnp.int32, (Q_ROWS, Q_ROWS), 0)
    col = lax.broadcasted_iota(jnp.int32, (Q_ROWS, Q_ROWS), 1)
    nt = (((1,), (1,)), ((), ()))

    n_blocks = seq_len // Q_ROWS

    def score(h, block_idx):
        start = block_idx * Q_ROWS
        q = q_s[h, start : start + Q_ROWS, :]
        s_diag = lax.dot_general(q, k_s[h, start : start + Q_ROWS, :], nt, preferred_element_type=f32)
        s_diag = jnp.where(col <= row, s_diag, -jnp.inf)
        if block_idx == 0:
            return (s_diag,)
        return s_diag, lax.dot_general(q, k_s[h, :start, :], nt, preferred_element_type=f32)

    def weigh(scores):
        peak = functools.reduce(jnp.maximum, [jnp.max(s, axis=-1, keepdims=True) for s in scores])
        weights = [jnp.exp2((s - peak) * exponent_scale) for s in scores]
        total = functools.reduce(jnp.add, [jnp.sum(e, axis=-1, keepdims=True) for e in weights])
        return [e.astype(jnp.bfloat16) for e in weights], total

    def mix(h, block_idx, weights, total):
        start = block_idx * Q_ROWS
        cols = pl.ds(pl.multiple_of(h * V_DIM, V_DIM), V_DIM)
        mixed = jnp.dot(weights[0], v_s[start : start + Q_ROWS, cols], preferred_element_type=f32)
        if block_idx:
            mixed = mixed + jnp.dot(weights[1], v_s[:start, cols], preferred_element_type=f32)
        o_ref[0, start : start + Q_ROWS, cols] = (mixed / total).astype(jnp.bfloat16)

    def attend(h, carry):
        tasks = [(h, block_idx) for block_idx in (*range(1, n_blocks, 2), *range((n_blocks - 1) // 2 * 2, -1, -2))]
        scores = {0: score(*tasks[0])}
        weights = {}
        for i in range(len(tasks)):
            if i + 1 < len(tasks):
                scores[i + 1] = score(*tasks[i + 1])
            if i:
                mix(*tasks[i - 1], *weights.pop(i - 1))
            weights[i] = weigh(scores.pop(i))
            if i + 1 == len(tasks):
                mix(*tasks[i], *weights.pop(i))

        return carry

    @pl.when(meta[0] == 1)
    def _():
        lax.fori_loop(0, seq_len // ROWS, project, 0)
        lax.fori_loop(0, n_heads, attend, 0)


def heads_call(meta, n_shards, n_req, first_req, tokens, c_kv, krp, wq, wukv, cos, sin, o_total, o_in):
    _, seq_len, d_model = tokens.shape
    kv_rank = c_kv.shape[-1]
    n_heads = wukv.shape[-1] // (NOPE_DIM + V_DIM)
    q_cols = wq.shape[-1]
    where_x = 1 + 2 * n_shards
    in_specs = [
        pl.BlockSpec((1, seq_len, d_model), lambda j, r, m: (m[where_x + r], 0, 0)),
        pl.BlockSpec((1, seq_len, kv_rank), lambda j, r, m: (r + first_req, 0, 0)),
        pl.BlockSpec((1, seq_len, 256), lambda j, r, m: (r + first_req, 0, 0)),
        pl.BlockSpec((1, d_model, q_cols), lambda j, r, m: (m[1 + j], 0, 0)),
        pl.BlockSpec((1, kv_rank, wukv.shape[-1]), lambda j, r, m: (m[1 + j], 0, 0)),
        pl.BlockSpec((seq_len, 128), lambda j, r, m: (0, 0)),
        pl.BlockSpec((seq_len, 128), lambda j, r, m: (0, 0)),
    ]
    operands = [meta, tokens, c_kv, krp, wq, wukv, cos, sin]
    aliases = {}
    out_shape = jax.ShapeDtypeStruct((c_kv.shape[0], seq_len, o_total), jnp.bfloat16)
    if o_in is not None:
        in_specs.append(pl.BlockSpec(memory_space=pl.ANY))
        operands.append(o_in)
        aliases = {8: 0}
    rows = n_shards * n_req * seq_len
    flops = 2 * rows * (d_model * q_cols + kv_rank * wukv.shape[-1] + n_heads * (seq_len // 2 + 128) * 512)
    return pl.pallas_call(
        functools.partial(heads_kernel, n_heads, seq_len, o_in is not None),
        out_shape=out_shape,
        grid_spec=pltpu.PrefetchScalarGridSpec(
            num_scalar_prefetch=1,
            grid=(n_shards, n_req),
            in_specs=in_specs,
            out_specs=pl.BlockSpec((1, seq_len, n_heads * V_DIM), lambda j, r, m: (r + first_req, 0, m[1 + n_shards + j])),
            scratch_shapes=[
                pltpu.VMEM((n_heads, seq_len, 256), jnp.bfloat16),
                pltpu.VMEM((n_heads, seq_len, 256), jnp.bfloat16),
                pltpu.VMEM((seq_len, n_heads * V_DIM), jnp.bfloat16),
            ],
        ),
        input_output_aliases=aliases,
        compiler_params=pltpu.CompilerParams(vmem_limit_bytes=60 * 1024 * 1024),
        cost_estimate=pl.CostEstimate(flops=flops, bytes_accessed=rows * d_model * 2, transcendentals=0),
    )(*operands)


def solution(mesh):
    n_tp = mesh.shape["t"]
    n_stage = mesh.shape["stage"]
    half_stage = n_stage // 2
    hand_pairs = [(s, s + half_stage) for s in range(half_stage)]
    back_pairs = [(s + half_stage, s) for s in range(half_stage)]
    twin_pairs = [(s, s ^ 1) for s in range(n_stage)]
    slot_spec = P(("dp", "stage"), None, None, None)
    cache_spec = P(("dp", "stage"), "t", None, None)

    def gather_shards(w_local):
        is_second = lax.axis_index("stage") % 2
        half = w_local.shape[0] // 2
        mine = lax.dynamic_slice_in_dim(w_local, is_second * half, half, axis=0)
        mine_all = lax.all_gather(mine, "t", axis=0, tiled=False)
        twin_all = lax.ppermute(mine_all, "stage", twin_pairs)
        low = jnp.where(is_second == 0, mine_all, twin_all)
        high = jnp.where(is_second == 0, twin_all, mine_all)
        return jnp.concatenate([low, high], axis=1)

    def layer(hidden, w_query, w_dkv, latent_gain, w_uk, w_uv, w_out):
        tokens = hidden[0]
        batch, seq_len, d_model = tokens.shape
        t_index = lax.axis_index("t")
        is_prompt = (lax.axis_index("stage") < half_stage).astype(jnp.int32)
        cos_tab, sin_tab = rope_tables(seq_len)
        cos4 = jnp.concatenate([cos_tab] * 4, axis=-1)
        sin4 = jnp.concatenate([-sin_tab, sin_tab, -sin_tab, sin_tab], axis=-1)

        n_away = batch // n_tp
        n_main = 3
        x_a = lax.ppermute(lax.dynamic_slice_in_dim(tokens, t_index * n_away, 1, axis=0), "stage", hand_pairs)
        x_b = lax.ppermute(lax.dynamic_slice_in_dim(tokens, t_index * n_away + 1, 1, axis=0), "stage", hand_pairs)

        n_heads = w_uk.shape[1] // NOPE_DIM
        by_head = w_query.reshape(d_model, n_heads, HEAD_DIM)
        wq_local = jnp.concatenate([by_head[:, :, :NOPE_DIM].reshape(d_model, -1), by_head[:, :, NOPE_DIM:].reshape(d_model, -1)], axis=1)
        wukv_local = jnp.concatenate([w_uk, w_uv], axis=1)
        wq_all = gather_shards(wq_local)
        wukv_all = gather_shards(wukv_local)
        wo_all = gather_shards(w_out)
        o_total = n_tp * n_heads * V_DIM
        wo_all = wo_all.reshape(o_total, d_model)

        odd = lax.rem(t_index, 2)
        neighbour = t_index + 1 - 2 * odd
        common = 2 * n_away * (1 - t_index // 2)
        order = jnp.stack([common + n_away + odd, common, common + 1, neighbour * n_away, neighbour * n_away + 1]).astype(jnp.int32)
        swapped_in = common + n_away + 1 - odd
        wd = jnp.concatenate([w_dkv, jnp.zeros((d_model, 128 - ROPE_DIM), w_dkv.dtype)], axis=1)
        gain = latent_gain.astype(jnp.float32)[None]
        one = jnp.ones((1,), jnp.int32)
        zero = jnp.zeros((1,), jnp.int32)
        prompt = is_prompt[None]
        here = t_index[None].astype(jnp.int32)
        away = lax.rem(t_index + 1 + jnp.arange(n_tp - 1, dtype=jnp.int32), n_tp)
        order_here = order * is_prompt
        tables = (cos4, sin4)

        def meta(*parts):
            return jnp.concatenate([p.astype(jnp.int32) for p in parts])

        def local_heads(active, xs, n_req, first, x, ckv, krp):
            return heads_call(meta(active, zero, here, xs), 1, n_req, first, x, ckv, krp, wq_local[None], wukv_local[None], *tables, o_total, None)

        def rest_heads(active, xs, n_req, first, x, ckv, krp, o_mix):
            return heads_call(meta(active, away, away, xs), n_tp - 1, n_req, first, x, ckv, krp, wq_all, wukv_all, *tables, o_total, o_mix)

        ckv, krp = latent_call(meta(prompt, prompt, order_here[:n_main]), n_main, tokens, None, wd, gain, *tables)
        o_swap = local_heads(prompt, order_here[:1], 1, 0, tokens, ckv, krp)
        o_main = local_heads(prompt, order_here[1:n_main], n_main - 1, 1, tokens, ckv, krp)

        def shared(slot, arrived):
            x, ckv_s, krp_s = latent_call(meta(one, prompt, order_here[slot : slot + 1]), 1, tokens, arrived, wd, gain, *tables)
            o_s = local_heads(one, zero, 1, 0, x, ckv_s, krp_s)
            o_s = rest_heads(one, zero, 1, 0, x, ckv_s, krp_s, o_s)
            y_s = out_call(meta(one, zero), 1, 0, o_s, wo_all, None)
            back = lax.ppermute(y_s, "stage", back_pairs)
            return y_s, back, jnp.concatenate([ckv_s, krp_s[..., :ROPE_DIM]], axis=-1)

        y_a, back_a, latent_a = shared(n_main, x_a)
        o_swap = rest_heads(prompt, order_here[:1], 1, 0, tokens, ckv, krp, o_swap)
        y_swap = out_call(meta(prompt, zero), 1, 0, o_swap, wo_all, None)
        from_neighbour = lax.ppermute(y_swap, "t", [(t, t ^ 1) for t in range(n_tp)])
        y_b, back_b, latent_b = shared(n_main + 1, x_b)
        o_main = rest_heads(prompt, order_here[1:n_main], n_main - 1, 1, tokens, ckv, krp, o_main)

        rows = jnp.zeros((batch, seq_len, d_model), jnp.bfloat16)
        rows = out_call(meta(prompt, order[1:n_main]), n_main - 1, 1, o_main, wo_all, rows)
        for y_s, slot in ((y_a, n_main), (y_b, n_main + 1), (y_swap, 0)):
            rows = lax.dynamic_update_slice_in_dim(rows, jnp.where(is_prompt == 1, y_s, jnp.zeros_like(y_s)), order[slot], axis=0)
        for back, place in ((back_a, t_index * n_away), (from_neighbour, swapped_in), (back_b, t_index * n_away + 1)):
            rows = lax.dynamic_update_slice_in_dim(rows, back, place, axis=0)
        latent = jnp.concatenate([latent_a, latent_b], axis=0)
        latent = jnp.where(is_prompt == 1, jnp.zeros_like(latent), latent)
        return rows[None], latent[None]

    return jax.shard_map(layer, mesh=mesh, in_specs=(slot_spec, P(None, "t"), P(None, None), P(None), P(None, "t"), P(None, "t"), P("t", None)), out_specs=(slot_spec, cache_spec), check_vma=False)
```

time: 2450 us -> 867 us (0.35)
  waiting for transfers between devices: 1820 us -> 151 us
  Pallas kernels: 0 us -> 527 us
  matrix products: 463 us -> 0 us
  local copies, waits for them, and re-layouts: 23.5 us -> 86.4 us
  other arithmetic: 120 us -> 68.2 us
    psum x1 -> x0, waiting for transfers between devices: 1560 us -> none  [device_step(): summed = lax.psum(part_sum.astype(jnp.bfloat16), 't')]
    pallas_call x0 -> x15, Pallas kernels: none -> 527 us  [the longest x8 378 us: heads_call(): pl.pallas_call(functools.partial(heads_kernel, n_heads, seq_len, o_in is...]
    dot_general x29 -> x0, matrix products: 463 us -> none  [the longest x8 148 us: causal_heads(): jnp.einsum('bqhe,bkhe->bhqk', q_nope[:, start_row:stop_row], k_nope[:, :s...]
    all_gather x1 -> x3, waiting for transfers between devices: 187 us -> 92.6 us  [gather_shards(): mine_all = lax.all_gather(mine, 't', axis=0, tiled=False)]
    reduce_sum x9 -> x0, other arithmetic: 67.9 us -> none  [the longest x8 67.3 us: causal_heads(): row_total = jnp.sum(weights, axis=-1)]
    broadcast_in_dim x1 -> x2, other arithmetic: 33.6 us -> 2.14 us  [the longest x1 2.14 us: local_heads(): wq_local[None]]
    concatenate x1 -> x17, other arithmetic: 1.93 us -> 26.6 us  [the longest x3 16.3 us: gather_shards(): return jnp.concatenate([low, high], axis=1)]
    ppermute x1 -> x8, waiting for transfers between devices: 74.3 us -> 58.6 us  [the longest x1 55.6 us: layer(): lax.ppermute(lax.dynamic_slice_in_dim(tokens, t_index * n_away + 1, 1, ax...]
  transfers between devices with their start and end apart: 3 -> 11, of which waited for: 3 -> 4; matrix products, arithmetic and copies ran while one was open for 2% -> 15% of each run, Pallas kernels for 0% -> 43%
where the time goes in v1:
time: 867 us; the launch traced here: 863 us
  Pallas kernels  527 us (61%)
  waiting for transfers between devices  151 us (17%)
  local copies, waits for them, and re-layouts  86.4 us (10%)
  other arithmetic  68.2 us (8%)
  starting transfers between devices  16.3 us (2%)
  between operations  14.3 us (2%)
    pallas_call x8, Pallas kernels, heads_call(): pl.pallas_call(functools.partial(heads_kernel, n_heads, seq_len, o_in is...  378 us
    pallas_call x4, Pallas kernels, out_call(): pl.pallas_call(functools.partial(out_kernel, d_model), out_shape=out_shap...  99.9 us
    all_gather x3, waiting for transfers between devices, gather_shards(): mine_all = lax.all_gather(mine, 't', axis=0, tiled=False)  92.6 us
    ppermute x1, waiting for transfers between devices, layer(): lax.ppermute(lax.dynamic_slice_in_dim(tokens, t_index * n_away + 1, 1, ax...  55.6 us
    pallas_call x3, Pallas kernels, latent_call(): pl.pallas_call(functools.partial(latent_kernel, kv_rank, arrived is not N...  48.8 us
    dynamic_update_slice x3, other arithmetic, layer(): lax.dynamic_update_slice_in_dim(rows, jnp.where(is_prompt == 1, y_s, jnp....  20.2 us
    dynamic_update_slice x3, local copies, waits for them, and re-layouts, layer(): rows = lax.dynamic_update_slice_in_dim(rows, back, place, axis=0)  20 us
    unnamed x38, local copies, waits for them, and re-layouts  19.7 us
  transfers between devices with their start and end apart: 11, of which 4 were waited for; matrix products, arithmetic and copies ran while one was open for 15% of the time, Pallas kernels for 43%

profile of v1, /device:TPU:0, one launch (start us, length us, event | category | flops | bytes accessed | tf_op | source)
XLA Modules:
  0.0 863.2 jit_solution(10468562845991797818)
XLA Ops:
  10.6 4.6 copy.17
  28.8 12.1 %dynamic-slice_bitcast_fusion = (bf16[1,1536,2048]{2,1,0:T(8,128)(2,1)}, bf16[1,1536,2048]{2,1,0:T(8,128)(2,1)}) fusion(bf16[1,8,1536,2048]{3,2,1,0:T(8,128)(2,1)} %param.7, s32[]{:T(128)S(6)} %select_n.126, s32[]{:T(128)S(6)} %select_n.123), kind=kLoop, calls=%fused_computation.8 | loop fusion | bytes 25165832 | tf_op jit(solution)/shard_map/dynamic_slice | solution.py:290
  40.9 7.7 collective-permute-start.3
  69.0 23.8 %shard_map.86 = (bf16[3,1536,512]{2,1,0:T(8,128)(2,1)}, bf16[3,1536,256]{2,1,0:T(8,128)(2,1)S(1)}) custom-call(s32[5]{0:T(128)S(1)} %pad_add_fusion.4.refs_0_, bf16[8,1536,2048]{2,1,0:T(8,128)(2,1)} %bitcast.44, bf16[2048,640]{1,0:T(8,128)(2,1)} %concatenate.84.refs_2_.refs_3_, f32[1,512]{1,0:T(1,128)S(1)} %bitcast.41, ...), custom_call_target="tpu_custom_call" | custom-call | flops 12079595520 | bytes 18874368 | tf_op jit(solution)/shard_map/pallas_call | solution.py:84
  94.2 39.4 %shard_map.87.refs_8_ = bf16[3,1536,2048]{2,1,0:T(8,128)(2,1)} custom-call(s32[5]{0:T(128)} %pad_add_fusion.5.refs_0_, bf16[8,1536,2048]{2,1,0:T(8,128)(2,1)} %bitcast.45, bf16[3,1536,512]{2,1,0:T(8,128)(2,1)} %get-tuple-element.10.refs_2_, bf16[3,1536,256]{2,1,0:T(8,128)(2,1)} %copy-done.6, bf16[1,2048,768]{2,1,0:T(8,128)(2,1)} %fusion.refs_4_, ...), custom_call_target="tpu_custom_call" | custom-call | flops 24159191040 | bytes 12582912 | tf_op jit(solution)/shard_map/pallas_call | solution.py:238
  136.3 23.1 %shard_map.98.refs_8_ = bf16[3,1536,2048]{2,1,0:T(8,128)(2,1)} custom-call(s32[4]{0:T(128)} %fusion.8.refs_0_, bf16[8,1536,2048]{2,1,0:T(8,128)(2,1)} %bitcast.46, bf16[3,1536,512]{2,1,0:T(8,128)(2,1)} %get-tuple-element.10.refs_2_, bf16[3,1536,256]{2,1,0:T(8,128)(2,1)} %copy-done.6, bf16[1,2048,768]{2,1,0:T(8,128)(2,1)} %fusion.refs_4_, ...), custom_call_target="tpu_custom_call" | custom-call | flops 12079595520 | bytes 6291456 | tf_op jit(solution)/shard_map/pallas_call | solution.py:238
  159.4 15.4 %all-gather.7.cloned.1.call-done = bf16[4096,768]{1,0:T(8,128)(2,1)} async-done(((bf16[1024,768]{1,0:T(8,128)(2,1)}), bf16[4096,768]{1,0:T(8,128)(2,1)}) %all-gather.7.cloned.1.call-update) | async-done | bytes 6291472 | tf_op jit(solution)/shard_map/all_gather | solution.py:272
  178.2 77.2 %all-gather.11.cloned.1.call-done = bf16[1024,2048]{1,0:T(8,128)(2,1)} async-done(((bf16[256,2048]{1,0:T(8,128)(2,1)}), bf16[1024,2048]{1,0:T(8,128)(2,1)}) %all-gather.11.cloned.1.call-update) | async-done | bytes 4194320 | tf_op jit(solution)/shard_map/all_gather | solution.py:272
  260.3 55.6 %collective-permute-done.4.refs_2_ = bf16[1,1536,2048]{2,1,0:T(8,128)(2,1)} collective-permute-done((bf16[1,1536,2048]{2,1,0:T(8,128)(2,1)}, bf16[1,1536,2048]{2,1,0:T(8,128)(2,1)}, u32[]{:S(2)}, u32[]{:S(2)}) %collective-permute-start.4) | collective-permute-done | bytes 6291488 | tf_op jit(solution)/shard_map/ppermute | solution.py:290
  315.9 12.5 %shard_map.94 = (bf16[1,1536,2048]{2,1,0:T(8,128)(2,1)}, bf16[1,1536,512]{2,1,0:T(8,128)(2,1)S(1)}, bf16[1,1536,256]{2,1,0:T(8,128)(2,1)S(1)}) custom-call(s32[3]{0:T(128)S(1)} %pad_add_fusion.9.refs_0_, bf16[8,1536,2048]{2,1,0:T(8,128)(2,1)} %bitcast.47, bf16[1,1536,2048]{2,1,0:T(8,128)(2,1)} %collective-permute-done.4.refs_2_, ...), custom_call_target="tpu_custom_call" | custom-call | flops 4026531840 | bytes 6291456 | tf_op jit(solution)/shard_map/pallas_call | solution.py:84
  329.3 12.5 %shard_map.90 = (bf16[1,1536,2048]{2,1,0:T(8,128)(2,1)}, bf16[1,1536,512]{2,1,0:T(8,128)(2,1)S(1)}, bf16[1,1536,256]{2,1,0:T(8,128)(2,1)S(1)}) custom-call(s32[3]{0:T(128)S(1)} %pad_add_fusion.7.refs_0_, bf16[8,1536,2048]{2,1,0:T(8,128)(2,1)} %bitcast.48, bf16[1,1536,2048]{2,1,0:T(8,128)(2,1)} %collective-permute-done.3.refs_2_, ...), custom_call_target="tpu_custom_call" | custom-call | flops 4026531840 | bytes 6291456 | tf_op jit(solution)/shard_map/pallas_call | solution.py:84
  345.9 6.1 copy.20
  352.0 23.4 %shard_map.91.refs_8_ = bf16[1,1536,2048]{2,1,0:T(8,128)(2,1)} custom-call(s32[4]{0:T(128)} %fusion.6.refs_0_, bf16[1,1536,2048]{2,1,0:T(8,128)(2,1)} %get-tuple-element.12.refs_1_, bf16[1,1536,512]{2,1,0:T(8,128)(2,1)} %copy-done.8, bf16[1,1536,256]{2,1,0:T(8,128)(2,1)} %copy-done.10, bf16[1,2048,768]{2,1,0:T(8,128)(2,1)} %fusion.refs_4_, ...), custom_call_target="tpu_custom_call" | custom-call | flops 12079595520 | bytes 6291456 | tf_op jit(solution)/shard_map/pallas_call | solution.py:238
  375.4 23.1 %shard_map.95.refs_8_ = bf16[1,1536,2048]{2,1,0:T(8,128)(2,1)} custom-call(s32[4]{0:T(128)} %fusion.6.refs_0_, bf16[1,1536,2048]{2,1,0:T(8,128)(2,1)} %get-tuple-element.15.refs_1_, bf16[1,1536,512]{2,1,0:T(8,128)(2,1)} %copy-done.7, bf16[1,1536,256]{2,1,0:T(8,128)(2,1)} %copy-done.9, bf16[1,2048,768]{2,1,0:T(8,128)(2,1)} %fusion.refs_4_, ...), custom_call_target="tpu_custom_call" | custom-call | flops 12079595520 | bytes 6291456 | tf_op jit(solution)/shard_map/pallas_call | solution.py:238
  398.5 5.8 broadcast_select_fusion.3
  404.3 8.4 pad_maximum_fusion.1
  412.7 5.4 broadcast_select_fusion.1
  418.1 5.5 pad_maximum_fusion.refs_4_
  423.6 55.1 %shard_map.92.refs_1_ = bf16[1,1536,2048]{2,1,0:T(8,128)(2,1)} custom-call(s32[8]{0:T(128)} %get-tuple-element.31.refs_0_, bf16[1,1536,2048]{2,1,0:T(8,128)(2,1)} %get-tuple-element.12.refs_1_, bf16[1,1536,512]{2,1,0:T(8,128)(2,1)} %copy-done.8, bf16[1,1536,256]{2,1,0:T(8,128)(2,1)} %copy-done.10, ...), custom_call_target="tpu_custom_call", output_to_operand_aliasing={{}: (8, {})} | custom-call | flops 36238786560 | bytes 18874368 | tf_op jit(solution)/shard_map/pallas_call | solution.py:238
  478.7 55.2 %shard_map.96.refs_1_ = bf16[1,1536,2048]{2,1,0:T(8,128)(2,1)} custom-call(s32[8]{0:T(128)} %get-tuple-element.31.refs_0_, bf16[1,1536,2048]{2,1,0:T(8,128)(2,1)} %get-tuple-element.15.refs_1_, bf16[1,1536,512]{2,1,0:T(8,128)(2,1)} %copy-done.7, bf16[1,1536,256]{2,1,0:T(8,128)(2,1)} %copy-done.9, ...), custom_call_target="tpu_custom_call", output_to_operand_aliasing={{}: (8, {})} | custom-call | flops 36238786560 | bytes 18874368 | tf_op jit(solution)/shard_map/pallas_call | solution.py:238
  533.9 21.2 %shard_map.93 = bf16[1,1536,2048]{2,1,0:T(8,128)(2,1)} custom-call(s32[2]{0:T(128)S(1)} %copy-done.11, bf16[1,1536,2048]{2,1,0:T(8,128)(2,1)} %shard_map.92.refs_1_, bf16[2048,2048]{1,0:T(8,128)(2,1)} %bitcast.52), custom_call_target="tpu_custom_call" | custom-call | flops 12884901888 | bytes 12582912 | tf_op jit(solution)/shard_map/pallas_call | solution.py:124
  555.1 21.2 %shard_map.97 = bf16[1,1536,2048]{2,1,0:T(8,128)(2,1)} custom-call(s32[2]{0:T(128)S(1)} %copy-done.11, bf16[1,1536,2048]{2,1,0:T(8,128)(2,1)} %shard_map.96.refs_1_, bf16[2048,2048]{1,0:T(8,128)(2,1)} %bitcast.53), custom_call_target="tpu_custom_call" | custom-call | flops 12884901888 | bytes 12582912 | tf_op jit(solution)/shard_map/pallas_call | solution.py:124
  577.7 55.0 %shard_map.99.refs_1_ = bf16[3,1536,2048]{2,1,0:T(8,128)(2,1)} custom-call(s32[8]{0:T(128)} %get-tuple-element.30.refs_0_, bf16[8,1536,2048]{2,1,0:T(8,128)(2,1)} %bitcast.49, bf16[3,1536,512]{2,1,0:T(8,128)(2,1)} %get-tuple-element.10.refs_2_, bf16[3,1536,256]{2,1,0:T(8,128)(2,1)} %copy-done.6, ...), custom_call_target="tpu_custom_call", output_to_operand_aliasing={{}: (8, {})} | custom-call | flops 36238786560 | bytes 18874368 | tf_op jit(solution)/shard_map/pallas_call | solution.py:238
  632.7 21.1 %shard_map.100 = bf16[1,1536,2048]{2,1,0:T(8,128)(2,1)} custom-call(s32[2]{0:T(128)S(1)} %pad_add_fusion.10.refs_0_, bf16[3,1536,2048]{2,1,0:T(8,128)(2,1)} %shard_map.99.refs_1_, bf16[2048,2048]{1,0:T(8,128)(2,1)} %bitcast.54), custom_call_target="tpu_custom_call" | custom-call | flops 12884901888 | bytes 12582912 | tf_op jit(solution)/shard_map/pallas_call | solution.py:124
  656.8 103.9 %shard_map.88.refs_1_ = bf16[3,1536,2048]{2,1,0:T(8,128)(2,1)} custom-call(s32[9]{0:T(128)} %pad_add_fusion.3.refs_0_, bf16[8,1536,2048]{2,1,0:T(8,128)(2,1)} %bitcast.50, bf16[3,1536,512]{2,1,0:T(8,128)(2,1)} %get-tuple-element.10.refs_2_, bf16[3,1536,256]{2,1,0:T(8,128)(2,1)} %copy-done.6, ...), custom_call_target="tpu_custom_call", output_to_operand_aliasing={{}: (8, {})} | custom-call | flops 72477573120 | bytes 37748736 | tf_op jit(solution)/shard_map/pallas_call | solution.py:238
  760.7 16.2 %broadcast_in_dim.54.refs_3_ = bf16[8,1536,2048]{2,1,0:T(8,128)(2,1)} broadcast(bf16[]{:T(256)} %constant.69.clone.1), dimensions={} | broadcast | bytes 50331648 | tf_op jit(solution)/shard_map/broadcast_in_dim | solution.py:345
  776.9 36.4 %shard_map.89 = bf16[8,1536,2048]{2,1,0:T(8,128)(2,1)} custom-call(s32[3]{0:T(128)S(1)} %pad_add_fusion.2.refs_0_, bf16[3,1536,2048]{2,1,0:T(8,128)(2,1)} %shard_map.88.refs_1_, bf16[2048,2048]{1,0:T(8,128)(2,1)} %bitcast.55, bf16[8,1536,2048]{2,1,0:T(8,128)(2,1)} %broadcast_in_dim.54.refs_3_), custom_call_target="tpu_custom_call", output_to_operand_aliasing={{}: (3, {})} | custom-call | flops 25769803776 | bytes 25165824 | tf_op jit(solution)/shard_map/pallas_call | solution.py:124
  813.3 7.8 bitcast_dynamic-update-slice_fusion.5
  821.1 7.8 bitcast_dynamic-update-slice_fusion.4
  833.5 6.6 bitcast_dynamic-update-slice_fusion.2
  840.1 6.8 bitcast_dynamic-update-slice_fusion.1
  849.8 6.6 bitcast_dynamic-update-slice_fusion
  (95 shorter events, 66.4 us)
Async XLA Ops:
  7.2 45.5 %copy-start = (bf16[512,2048]{1,0:T(8,128)(2,1)S(1)}, bf16[512,2048]{1,0:T(8,128)(2,1)}, u32[]{:S(2)}) copy-start(bf16[512,2048]{1,0:T(8,128)(2,1)} %param.13) | copy-start | bytes 6291460
  7.2 126.5 %all-gather.9.cloned.1.call-start = ((), (), s32[]{:S(2)}) async-start(), calls=%async_computation.1 | async-start | bytes 2621440 | tf_op jit(solution)/shard_map/all_gather | solution.py:272
  9.6 11.1 %copy-start.13 = (bf16[512,1024]{1,0:T(8,128)(2,1)}, bf16[512,1024]{1,0:T(8,128)(2,1)S(1)}, u32[]{:S(2)}) copy-start(bf16[512,1024]{1,0:T(8,128)(2,1)S(1)} %constant_dynamic-update-slice_fusion) | copy-start | bytes 3145732
  10.5 164.3 %all-gather.7.cloned.1.call-start = ((), (), s32[]{:S(2)}) async-start(), calls=%async_computation | async-start | bytes 7864320 | tf_op jit(solution)/shard_map/all_gather | solution.py:272
  28.7 226.6 %all-gather.11.cloned.1.call-start = ((), (), s32[]{:S(2)}) async-start(), calls=%async_computation.2 | async-start | bytes 5242880 | tf_op jit(solution)/shard_map/all_gather | solution.py:272
  40.9 17.6 %copy-start.14 = (bf16[512]{0:T(512)(128)(2,1)S(1)}, bf16[512]{0:T(512)(128)(2,1)}, u32[]{:S(2)}) copy-start(bf16[512]{0:T(512)(128)(2,1)} %param.10) | copy-start | bytes 3076
  40.9 288.5 %collective-permute-start.3 = (bf16[1,1536,2048]{2,1,0:T(8,128)(2,1)}, bf16[1,1536,2048]{2,1,0:T(8,128)(2,1)}, u32[]{:S(2)}, u32[]{:S(2)}) collective-permute-start(bf16[1,1536,2048]{2,1,0:T(8,128)(2,1)} %get-tuple-element.23), channel_id=1, source_target_pairs={{0,2},{1,3},{4,6},{5,7},{8,10},{9,11},{12,14},{13,15},{16,18},{17,... | collective-permute-start | bytes 18874376 | tf_op jit(solution)/shard_map/ppermute | solution.py:289
  48.6 267.3 %collective-permute-start.4 = (bf16[1,1536,2048]{2,1,0:T(8,128)(2,1)}, bf16[1,1536,2048]{2,1,0:T(8,128)(2,1)}, u32[]{:S(2)}, u32[]{:S(2)}) collective-permute-start(bf16[1,1536,2048]{2,1,0:T(8,128)(2,1)} %get-tuple-element.22), channel_id=1, source_target_pairs={{0,2},{1,3},{4,6},{5,7},{8,10},{9,11},{12,14},{13,15},{16,18},{17,... | collective-permute-start | bytes 18874376 | tf_op jit(solution)/shard_map/ppermute | solution.py:290
  58.4 7.8 copy-start.12
  66.3 26.5 %copy-start.2 = (f32[1536,128]{1,0:T(8,128)}, f32[1536,128]{1,0:T(8,128)S(1)}, u32[]{:S(2)}) copy-start(f32[1536,128]{1,0:T(8,128)S(1)} %get-tuple-element.38.refs_4_.refs_6_.refs_5_) | copy-start | bytes 2359300
  66.3 26.5 %copy-start.4 = (f32[1536,128]{1,0:T(8,128)}, f32[1536,128]{1,0:T(8,128)S(1)}, u32[]{:S(2)}) copy-start(f32[1536,128]{1,0:T(8,128)S(1)} %get-tuple-element.39.refs_5_.refs_7_.refs_6_) | copy-start | bytes 2359300
  92.8 1.4 copy-start.6
  133.6 121.7 %collective-permute-start.1 = (bf16[4,256,1024]{2,1,0:T(8,128)(2,1)}, bf16[4,256,1024]{2,1,0:T(8,128)(2,1)}, u32[]{:S(2)}, u32[]{:S(2)}) collective-permute-start(bf16[4,256,1024]{2,1,0:T(8,128)(2,1)} %bitcast.70), channel_id=1, source_target_pairs={{0,1},{1,0},{2,3},{3,2},{4,5},{5,4},{6,7},{7,6},{8,9},{9,8},{10,11... | collective-permute-start | bytes 6291464 | tf_op jit(solution)/shard_map/ppermute | solution.py:273
  174.8 237.9 %collective-permute-start = (bf16[4,1024,768]{2,1,0:T(8,128)(2,1)}, bf16[4,1024,768]{2,1,0:T(8,128)(2,1)}, u32[]{:S(2)}, u32[]{:S(2)}) collective-permute-start(bf16[4,1024,768]{2,1,0:T(8,128)(2,1)} %bitcast.61), channel_id=1, source_target_pairs={{0,1},{1,0},{2,3},{3,2},{4,5},{5,4},{6,7},{7,6},{8,9},{9,8},{10,11... | collective-permute-start | bytes 18874376 | tf_op jit(solution)/shard_map/ppermute | solution.py:273
  255.3 143.2 %collective-permute-start.2 = (bf16[4,256,2048]{2,1,0:T(8,128)(2,1)}, bf16[4,256,2048]{2,1,0:T(8,128)(2,1)}, u32[]{:S(2)}, u32[]{:S(2)}) collective-permute-start(bf16[4,256,2048]{2,1,0:T(8,128)(2,1)} %bitcast.67), channel_id=1, source_target_pairs={{0,1},{1,0},{2,3},{3,2},{4,5},{5,4},{6,7},{7,6},{8,9},{9,8},{10,11... | collective-permute-start | bytes 12582920 | tf_op jit(solution)/shard_map/ppermute | solution.py:273
  257.8 58.0 %copy-start.3 = (f32[1536,128]{1,0:T(8,128)S(1)}, f32[1536,128]{1,0:T(8,128)}, u32[]{:S(2)}) copy-start(f32[1536,128]{1,0:T(8,128)} %copy-done.2) | copy-start | bytes 2359300
  257.9 58.0 %copy-start.5 = (f32[1536,128]{1,0:T(8,128)S(1)}, f32[1536,128]{1,0:T(8,128)}, u32[]{:S(2)}) copy-start(f32[1536,128]{1,0:T(8,128)} %copy-done.4) | copy-start | bytes 2359300
  328.4 0.9 copy-start.9
  328.4 13.5 %copy-start.7 = (bf16[1,1536,512]{2,1,0:T(8,128)(2,1)}, bf16[1,1536,512]{2,1,0:T(8,128)(2,1)S(1)}, u32[]{:S(2)}) copy-start(bf16[1,1536,512]{2,1,0:T(8,128)(2,1)S(1)} %get-tuple-element.16.refs_2_) | copy-start | bytes 4718596
  341.8 1.1 copy-start.8
  341.8 1.4 copy-start.10
  478.7 55.2 %copy-start.11 = (s32[2]{0:T(128)S(1)}, s32[2]{0:T(128)}, u32[]{:S(2)}) copy-start(s32[2]{0:T(128)} %constant.77.clone.1.refs_0_) | copy-start | bytes 28
  576.2 257.3 %collective-permute-start.5 = (bf16[1,1536,2048]{2,1,0:T(8,128)(2,1)}, bf16[1,1536,2048]{2,1,0:T(8,128)(2,1)}, u32[]{:S(2)}, u32[]{:S(2)}) collective-permute-start(bf16[1,1536,2048]{2,1,0:T(8,128)(2,1)} %shard_map.93), channel_id=1, source_target_pairs={{2,0},{3,1},{6,4},{7,5},{10,8},{11,9},{14,12},{15,13},{18,16},{19,... | collective-permute-start | bytes 18874376 | tf_op jit(solution)/shard_map/ppermute | solution.py:335
  653.9 186.2 %collective-permute-start.6 = (bf16[1,1536,2048]{2,1,0:T(8,128)(2,1)}, bf16[1,1536,2048]{2,1,0:T(8,128)(2,1)}, u32[]{:S(2)}, u32[]{:S(2)}) collective-permute-start(bf16[1,1536,2048]{2,1,0:T(8,128)(2,1)} %shard_map.100), channel_id=1, source_target_pairs={{0,4},{4,0},{8,12},{12,8},{1,5},{5,1},{9,13},{13,9},{2,6},{6,2},{1... | collective-permute-start | bytes 18874376 | tf_op jit(solution)/shard_map/ppermute | solution.py:341
  655.5 194.3 %collective-permute-start.7 = (bf16[1,1536,2048]{2,1,0:T(8,128)(2,1)}, bf16[1,1536,2048]{2,1,0:T(8,128)(2,1)}, u32[]{:S(2)}, u32[]{:S(2)}) collective-permute-start(bf16[1,1536,2048]{2,1,0:T(8,128)(2,1)} %shard_map.97), channel_id=1, source_target_pairs={{2,0},{3,1},{6,4},{7,5},{10,8},{11,9},{14,12},{15,13},{18,16},{19,... | collective-permute-start | bytes 18874376 | tf_op jit(solution)/shard_map/ppermute | solution.py:335
  813.3 15.7 %slice-start = ((s8[6291456]{0:T(1024)(128)(4,1)}), s8[4194304]{0:T(1024)(128)(4,1)S(1)}, s32[]{:S(2)}) async-start(s8[6291456]{0:T(1024)(128)(4,1)} %bitcast.59), calls=%async_computation.3 | async-start | bytes 8388608
  821.1 7.8 slice-start.1
  840.1 16.3 %copy-start.1 = (bf16[512,2048]{1,0:T(8,128)(2,1)S(1)}, bf16[512,2048]{1,0:T(8,128)(2,1)}, u32[]{:S(2)}) copy-start(bf16[512,2048]{1,0:T(8,128)(2,1)} %param.13) | copy-start | bytes 6291460
Sparse Core Ops, SparseCore 0:
  10.6 48.3 all-gather.8
  60.6 114.1 all-gather.6
  176.4 78.8 all-gather.10

commit v2 on v1

v2 whole, which is shorter than its diff:
```python
import functools

import jax
import jax.numpy as jnp
from jax import lax
from jax.experimental import pallas as pl
from jax.experimental.pallas import tpu as pltpu
from jax.sharding import PartitionSpec as P


NOPE_DIM = 128
ROPE_DIM = 64
V_DIM = 128
HEAD_DIM = NOPE_DIM + ROPE_DIM
NORM_EPS = 1e-6
ROPE_BASE = 10000.0
LOG2E = 1.4426950408889634
ROWS = 512
Q_ROWS = 256


def rope_tables(seq_len):
    half_dim = ROPE_DIM // 2
    positions = jnp.arange(seq_len, dtype=jnp.float32)
    inv_freq = ROPE_BASE ** (-jnp.arange(half_dim, dtype=jnp.float32) / half_dim)
    angles = positions[:, None] * inv_freq[None, :]
    return jnp.cos(angles), jnp.sin(angles)


def swap_halves(w, is_low):
    return jnp.where(is_low, pltpu.roll(w, 96, 1), pltpu.roll(w, 32, 1))


def latent_kernel(kv_rank, meta, x_ref, wd_ref, gain_ref, cos_ref, sin_ref, ckv_ref, krp_ref):
    f32 = jnp.float32

    def body():
        comp = jnp.dot(x_ref[0], wd_ref[...], preferred_element_type=f32).astype(jnp.bfloat16)
        raw = comp[:, :kv_rank].astype(f32)
        inv_rms = lax.rsqrt(jnp.mean(raw * raw, axis=-1, keepdims=True) + NORM_EPS)
        ckv_ref[0] = (raw * inv_rms * gain_ref[...]).astype(jnp.bfloat16)
        w = comp[:, kv_rank:].astype(f32)
        lane = lax.broadcasted_iota(jnp.int32, w.shape, 1)
        is_low = (lane % ROPE_DIM) < ROPE_DIM // 2
        roped = w * cos_ref[...] + swap_halves(w, is_low) * sin_ref[...]
        krp_ref[0, :, :128] = roped.astype(jnp.bfloat16)
        krp_ref[0, :, 128:] = pltpu.roll(roped, 64, 1).astype(jnp.bfloat16)

    pl.when(meta[0] == 1)(body)


def latent_call(meta, n_req, tokens, w_dkv, gain, cos, sin):
    _, seq_len, d_model = tokens.shape
    kv_rank = gain.shape[-1]
    in_specs = [pl.BlockSpec((1, ROWS, d_model), lambda r, i, m: (m[1 + r], i * m[0], 0))]
    operands = [meta, tokens]
    out_shape = [
        jax.ShapeDtypeStruct((n_req, seq_len, kv_rank), jnp.bfloat16),
        jax.ShapeDtypeStruct((n_req, seq_len, 256), jnp.bfloat16),
    ]
    out_specs = [
        pl.BlockSpec((1, ROWS, kv_rank), lambda r, i, m: (r * m[0], i * m[0], 0)),
        pl.BlockSpec((1, ROWS, 256), lambda r, i, m: (r * m[0], i * m[0], 0)),
    ]
    in_specs += [
        pl.BlockSpec(w_dkv.shape, lambda r, i, m: (0, 0)),
        pl.BlockSpec((1, kv_rank), lambda r, i, m: (0, 0)),
        pl.BlockSpec((ROWS, 128), lambda r, i, m: (i, 0)),
        pl.BlockSpec((ROWS, 128), lambda r, i, m: (i, 0)),
    ]
    return pl.pallas_call(
        functools.partial(latent_kernel, kv_rank),
        out_shape=out_shape,
        grid_spec=pltpu.PrefetchScalarGridSpec(num_scalar_prefetch=1, grid=(n_req, seq_len // ROWS), in_specs=in_specs, out_specs=out_specs),
        compiler_params=pltpu.CompilerParams(vmem_limit_bytes=48 * 1024 * 1024),
        cost_estimate=pl.CostEstimate(flops=2 * n_req * seq_len * d_model * w_dkv.shape[1], bytes_accessed=n_req * seq_len * d_model * 2, transcendentals=0),
    )(*operands, w_dkv, gain, cos, sin)


def out_kernel(n_cols, meta, o_ref, mine_ref, twin_ref, *refs):
    y_ref, w_ref = refs[-2:]
    n_shards, half, _ = mine_ref.shape

    @pl.when(meta[0] * (pl.program_id(0) == 0) * (pl.program_id(1) == 0) == 1)
    def _():
        for j in range(n_shards):
            for part_ref, second in ((mine_ref, meta[1]), (twin_ref, 1 - meta[1])):
                w_ref[pl.ds(pl.multiple_of((2 * j + second) * half, half), half), :] = part_ref[j]

    def multiply(n, carry):
        cols = pl.ds(pl.multiple_of(n * ROWS, ROWS), ROWS)
        y_ref[0, :, cols] = jnp.dot(o_ref[0], w_ref[:, cols], preferred_element_type=jnp.float32).astype(jnp.bfloat16)
        return carry

    @pl.when(meta[0] == 1)
    def _():
        lax.fori_loop(0, n_cols // ROWS, multiply, 0)

    @pl.when(meta[0] != 1)
    def _():
        y_ref[...] = jnp.zeros_like(y_ref)


def out_call(meta, n_req, first_req, o_mix, w_mine, w_twin, n_rows, idle_rows):
    _, seq_len, depth = o_mix.shape
    d_model = w_mine.shape[-1]
    in_specs = [
        pl.BlockSpec((1, ROWS, depth), lambda r, i, m: ((r + first_req) * m[0], i * m[0], 0)),
        pl.BlockSpec(w_mine.shape, lambda r, i, m: (0, 0, 0)),
        pl.BlockSpec(w_twin.shape, lambda r, i, m: (0, 0, 0)),
    ]
    operands = [meta, o_mix, w_mine, w_twin]
    block = (1, ROWS, d_model)
    return pl.pallas_call(
        functools.partial(out_kernel, d_model),
        out_shape=jax.ShapeDtypeStruct((n_rows, seq_len, d_model), jnp.bfloat16),
        grid_spec=pltpu.PrefetchScalarGridSpec(num_scalar_prefetch=1, grid=(n_req, seq_len // ROWS), in_specs=in_specs, out_specs=pl.BlockSpec(block, lambda r, i, m: (m[2 + r], i if idle_rows else i * m[0], 0)), scratch_shapes=[pltpu.VMEM((depth, d_model), jnp.bfloat16)]),
        compiler_params=pltpu.CompilerParams(vmem_limit_bytes=48 * 1024 * 1024),
        cost_estimate=pl.CostEstimate(flops=2 * n_req * seq_len * depth * d_model, bytes_accessed=n_req * seq_len * d_model * 4, transcendentals=0),
    )(*operands)


def heads_kernel(n_heads, seq_len, chained, *refs):
    if chained:
        meta, x_ref, ckv_ref, krp_ref, mine_ref, twin_ref, wukv_ref, cos_ref, sin_ref, _, o_ref, q_s, k_s, v_s, wq_s = refs
    else:
        meta, x_ref, ckv_ref, krp_ref, mine_ref, twin_ref, wukv_ref, cos_ref, sin_ref, o_ref, q_s, k_s, v_s, wq_s = refs
    nope_cols = n_heads * NOPE_DIM
    f32 = jnp.float32

    def project(block_idx, carry):
        rows = pl.ds(pl.multiple_of(block_idx * ROWS, ROWS), ROWS)
        lat = ckv_ref[0, rows, :]
        k_nope = jnp.dot(lat, wukv_ref[0, :, :nope_cols], preferred_element_type=f32).astype(jnp.bfloat16)
        v_s[rows, :] = jnp.dot(lat, wukv_ref[0, :, nope_cols:], preferred_element_type=f32).astype(jnp.bfloat16)
        x = x_ref[0, rows, :]
        q_nope = jnp.dot(x, wq_s[:, :nope_cols], preferred_element_type=f32).astype(jnp.bfloat16)
        q_rope = jnp.dot(x, wq_s[:, nope_cols:], preferred_element_type=f32).astype(jnp.bfloat16)
        cos, sin = cos_ref[rows, :], sin_ref[rows, :]
        lane = lax.broadcasted_iota(jnp.int32, (ROWS, 128), 1)
        is_low = (lane % ROPE_DIM) < ROPE_DIM // 2
        for h in range(n_heads):
            if h % 2 == 0:
                w = q_rope[:, h * ROPE_DIM : h * ROPE_DIM + 128].astype(f32)
                roped = (w * cos + swap_halves(w, is_low) * sin).astype(jnp.bfloat16)
            q_s[h, rows, :NOPE_DIM] = q_nope[:, h * NOPE_DIM : (h + 1) * NOPE_DIM]
            q_s[h, rows, NOPE_DIM:] = roped
            k_s[h, rows, :NOPE_DIM] = k_nope[:, h * NOPE_DIM : (h + 1) * NOPE_DIM]
            k_s[h, rows, NOPE_DIM:] = krp_ref[0, rows, (h % 2) * 128 : (h % 2 + 1) * 128]
        return carry

    exponent_scale = HEAD_DIM ** -0.5 * LOG2E
    row = lax.broadcasted_iota(jnp.int32, (Q_ROWS, Q_ROWS), 0)
    col = lax.broadcasted_iota(jnp.int32, (Q_ROWS, Q_ROWS), 1)
    nt = (((1,), (1,)), ((), ()))

    n_blocks = seq_len // Q_ROWS

    def score(h, block_idx):
        start = block_idx * Q_ROWS
        q = q_s[h, start : start + Q_ROWS, :]
        s_diag = lax.dot_general(q, k_s[h, start : start + Q_ROWS, :], nt, preferred_element_type=f32)
        s_diag = jnp.where(col <= row, s_diag, -jnp.inf)
        if block_idx == 0:
            return (s_diag,)
        return s_diag, lax.dot_general(q, k_s[h, :start, :], nt, preferred_element_type=f32)

    def weigh(scores):
        peak = functools.reduce(jnp.maximum, [jnp.max(s, axis=-1, keepdims=True) for s in scores])
        weights = [jnp.exp2((s - peak) * exponent_scale) for s in scores]
        total = functools.reduce(jnp.add, [jnp.sum(e, axis=-1, keepdims=True) for e in weights])
        return [e.astype(jnp.bfloat16) for e in weights], total

    def mix(h, block_idx, weights, total):
        start = block_idx * Q_ROWS
        cols = pl.ds(pl.multiple_of(h * V_DIM, V_DIM), V_DIM)
        mixed = jnp.dot(weights[0], v_s[start : start + Q_ROWS, cols], preferred_element_type=f32)
        if block_idx:
            mixed = mixed + jnp.dot(weights[1], v_s[:start, cols], preferred_element_type=f32)
        o_ref[0, start : start + Q_ROWS, cols] = (mixed / total).astype(jnp.bfloat16)

    def attend(h, carry):
        tasks = [(h, block_idx) for block_idx in (*range(1, n_blocks, 2), *range((n_blocks - 1) // 2 * 2, -1, -2))]
        scores = {0: score(*tasks[0])}
        weights = {}
        for i in range(len(tasks)):
            if i + 1 < len(tasks):
                scores[i + 1] = score(*tasks[i + 1])
            if i:
                mix(*tasks[i - 1], *weights.pop(i - 1))
            weights[i] = weigh(scores.pop(i))
            if i + 1 == len(tasks):
                mix(*tasks[i], *weights.pop(i))

        return carry

    half = mine_ref.shape[1]

    @pl.when(meta[0] * (pl.program_id(1) == 0) == 1)
    def _():
        wq_s[pl.ds(pl.multiple_of(meta[1] * half, half), half), :] = mine_ref[0]
        wq_s[pl.ds(pl.multiple_of((1 - meta[1]) * half, half), half), :] = twin_ref[0]

    @pl.when(meta[0] == 1)
    def _():
        lax.fori_loop(0, seq_len // ROWS, project, 0)
        lax.fori_loop(0, n_heads, attend, 0)


def heads_call(meta, n_shards, n_req, first_req, tokens, c_kv, krp, wq_mine, wq_twin, twin_block, wukv, cos, sin, o_total, o_in):
    _, seq_len, d_model = tokens.shape
    kv_rank = c_kv.shape[-1]
    n_heads = wukv.shape[-1] // (NOPE_DIM + V_DIM)
    q_cols = wq_mine.shape[-1]
    where_x = 2 + 2 * n_shards
    in_specs = [
        pl.BlockSpec((1, seq_len, d_model), lambda j, r, m: (m[where_x + r], 0, 0)),
        pl.BlockSpec((1, seq_len, kv_rank), lambda j, r, m: ((r + first_req) * m[0], 0, 0)),
        pl.BlockSpec((1, seq_len, 256), lambda j, r, m: ((r + first_req) * m[0], 0, 0)),
        pl.BlockSpec((1, d_model // 2, q_cols), lambda j, r, m: (m[2 + j], 0, 0)),
        pl.BlockSpec((1, d_model // 2, q_cols), lambda j, r, m: (m[2 + j], twin_block, 0)),
        pl.BlockSpec((1, kv_rank, wukv.shape[-1]), lambda j, r, m: (m[2 + j], 0, 0)),
        pl.BlockSpec((seq_len, 128), lambda j, r, m: (0, 0)),
        pl.BlockSpec((seq_len, 128), lambda j, r, m: (0, 0)),
    ]
    operands = [meta, tokens, c_kv, krp, wq_mine, wq_twin, wukv, cos, sin]
    aliases = {}
    out_shape = jax.ShapeDtypeStruct((c_kv.shape[0], seq_len, o_total), jnp.bfloat16)
    if o_in is not None:
        in_specs.append(pl.BlockSpec(memory_space=pl.ANY))
        operands.append(o_in)
        aliases = {9: 0}
    rows = n_shards * n_req * seq_len
    flops = 2 * rows * (d_model * q_cols + kv_rank * wukv.shape[-1] + n_heads * (seq_len // 2 + 128) * 512)
    return pl.pallas_call(
        functools.partial(heads_kernel, n_heads, seq_len, o_in is not None),
        out_shape=out_shape,
        grid_spec=pltpu.PrefetchScalarGridSpec(
            num_scalar_prefetch=1,
            grid=(n_shards, n_req),
            in_specs=in_specs,
            out_specs=pl.BlockSpec((1, seq_len, n_heads * V_DIM), lambda j, r, m: ((r + first_req) * m[0], 0, m[2 + n_shards + j])),
            scratch_shapes=[
                pltpu.VMEM((n_heads, seq_len, 256), jnp.bfloat16),
                pltpu.VMEM((n_heads, seq_len, 256), jnp.bfloat16),
                pltpu.VMEM((seq_len, n_heads * V_DIM), jnp.bfloat16),
                pltpu.VMEM((d_model, q_cols), jnp.bfloat16),
            ],
        ),
        input_output_aliases=aliases,
        compiler_params=pltpu.CompilerParams(vmem_limit_bytes=60 * 1024 * 1024),
        cost_estimate=pl.CostEstimate(flops=flops, bytes_accessed=rows * d_model * 2, transcendentals=0),
    )(*operands)


def solution(mesh):
    n_tp = mesh.shape["t"]
    n_stage = mesh.shape["stage"]
    half_stage = n_stage // 2
    hand_pairs = [(s, s + half_stage) for s in range(half_stage)]
    back_pairs = [(s + half_stage, s) for s in range(half_stage)]
    twin_pairs = [(s, s ^ 1) for s in range(n_stage)]
    slot_spec = P(("dp", "stage"), None, None, None)
    cache_spec = P(("dp", "stage"), "t", None, None)

    def gather_shards(w_local):
        is_second = lax.axis_index("stage") % 2
        half = w_local.shape[0] // 2
        mine = lax.dynamic_slice_in_dim(w_local, is_second * half, half, axis=0)
        mine_all = lax.all_gather(mine, "t", axis=0, tiled=False)
        twin_all = lax.ppermute(mine_all, "stage", twin_pairs)
        return mine_all, twin_all

    def join_halves(mine_all, twin_all):
        is_second = lax.axis_index("stage") % 2
        low = jnp.where(is_second == 0, mine_all, twin_all)
        high = jnp.where(is_second == 0, twin_all, mine_all)
        return jnp.concatenate([low, high], axis=1)

    def layer(hidden, w_query, w_dkv, latent_gain, w_uk, w_uv, w_out):
        tokens = hidden[0]
        batch, seq_len, d_model = tokens.shape
        t_index = lax.axis_index("t")
        is_prompt = (lax.axis_index("stage") < half_stage).astype(jnp.int32)
        cos_tab, sin_tab = rope_tables(seq_len)
        cos4 = jnp.concatenate([cos_tab] * 4, axis=-1)
        sin4 = jnp.concatenate([-sin_tab, sin_tab, -sin_tab, sin_tab], axis=-1)

        n_away = batch // n_tp
        n_main = batch - 2 * n_away
        x_a = lax.ppermute(lax.dynamic_slice_in_dim(tokens, t_index * n_away, 1, axis=0), "stage", hand_pairs)
        x_b = lax.ppermute(lax.dynamic_slice_in_dim(tokens, t_index * n_away + 1, 1, axis=0), "stage", hand_pairs)

        n_heads = w_uk.shape[1] // NOPE_DIM
        by_head = w_query.reshape(d_model, n_heads, HEAD_DIM)
        wq_local = jnp.concatenate([by_head[:, :, :NOPE_DIM].reshape(d_model, -1), by_head[:, :, NOPE_DIM:].reshape(d_model, -1)], axis=1)
        wukv_local = jnp.concatenate([w_uk, w_uv], axis=1)
        wq_halves = gather_shards(wq_local)
        wukv_all = join_halves(*gather_shards(wukv_local))
        wo_halves = gather_shards(w_out)
        o_total = n_tp * n_heads * V_DIM

        odd = lax.rem(t_index, 2)
        neighbour = t_index + 1 - 2 * odd
        common = 2 * n_away * (1 - t_index // 2)
        order = jnp.stack([common + 2 + odd, common + odd, neighbour * n_away, neighbour * n_away + 1]).astype(jnp.int32)
        swapped_in = (common + 3 - odd, common + 1 - odd)
        wd = jnp.concatenate([w_dkv, jnp.zeros((d_model, 128 - ROPE_DIM), w_dkv.dtype)], axis=1)
        gain = latent_gain.astype(jnp.float32)[None]
        zero = jnp.zeros((1,), jnp.int32)
        prompt = is_prompt[None]
        here = t_index[None].astype(jnp.int32)
        away = lax.rem(t_index + 1 + jnp.arange(n_tp - 1, dtype=jnp.int32), n_tp)
        order_here = order * is_prompt
        cache_side = 1 - prompt
        second = lax.rem(lax.axis_index("stage"), 2)[None]
        tables = (cos4, sin4)

        def meta(*parts):
            return jnp.concatenate([p.astype(jnp.int32) for p in parts])

        def local_heads(active, xs, n_req, first, x, ckv, krp):
            return heads_call(meta(active, zero, zero, here, xs), 1, n_req, first, x, ckv, krp, wq_local[None], wq_local[None], 1, wukv_local[None], *tables, o_total, None)

        def rest_heads(active, xs, n_req, first, x, ckv, krp, o_mix):
            places = jnp.where(active == 1, away, away[:1])
            return heads_call(meta(active, second, places, places, xs), n_tp - 1, n_req, first, x, ckv, krp, *wq_halves, 0, wukv_all, *tables, o_total, o_mix)

        ckv, krp = latent_call(meta(prompt, order_here), n_main, tokens, wd, gain, *tables)
        o_swap = local_heads(prompt, order_here[:1], 1, 0, tokens, ckv, krp)
        o_swap2 = local_heads(prompt, order_here[1:2], 1, 1, tokens, ckv, krp)
        o_main = local_heads(prompt, order_here[2:], n_main - 2, 2, tokens, ckv, krp)

        def on_cache_side(x):
            ckv_s, krp_s = latent_call(meta(cache_side, zero), 1, x, wd, gain, *tables)
            o_s = local_heads(cache_side, zero, 1, 0, x, ckv_s, krp_s)
            o_s = rest_heads(cache_side, zero, 1, 0, x, ckv_s, krp_s, o_s)
            y_s = out_call(meta(cache_side, second, zero), 1, 0, o_s, *wo_halves, 1, False)
            back = lax.ppermute(y_s, "stage", back_pairs)
            return back, jnp.concatenate([ckv_s, krp_s[..., :ROPE_DIM]], axis=-1)

        back_a, latent_a = on_cache_side(x_a)

        def for_both(place, o_s):
            o_s = rest_heads(prompt, order_here[place : place + 1], 1, place, tokens, ckv, krp, o_s)
            y_s = out_call(meta(prompt, second, zero), 1, place, o_s, *wo_halves, 1, True)
            return y_s, lax.ppermute(y_s, "t", [(t, t ^ 1) for t in range(n_tp)])

        y_swap, from_swap = for_both(0, o_swap)
        y_swap2, from_swap2 = for_both(1, o_swap2)
        back_b, latent_b = on_cache_side(x_b)
        o_main = rest_heads(prompt, order_here[2:], n_main - 2, 2, tokens, ckv, krp, o_main)

        rows = out_call(meta(prompt, second, order[2:]), n_main - 2, 2, o_main, *wo_halves, batch, True)
        placed = ((y_swap, order[0]), (y_swap2, order[1]), (back_a, t_index * n_away), (from_swap, swapped_in[0]), (from_swap2, swapped_in[1]), (back_b, t_index * n_away + 1))
        for piece, place in placed:
            rows = lax.dynamic_update_slice_in_dim(rows, piece, place, axis=0)
        latent = jnp.concatenate([latent_a, latent_b], axis=0)
        latent = jnp.where(is_prompt == 1, jnp.zeros_like(latent), latent)
        return rows[None], latent[None]

    return jax.shard_map(layer, mesh=mesh, in_specs=(slot_spec, P(None, "t"), P(None, None), P(None), P(None, "t"), P(None, "t"), P("t", None)), out_specs=(slot_spec, cache_spec), check_vma=False)
```

time: 867 us -> 866 us (level)
  the two profiles are of different devices: /device:TPU:0 before, /device:TPU:12 now
where the time goes in v2:
time: 866 us; the launch traced here: 862 us
  waiting for transfers between devices  427 us (49%)
  Pallas kernels  289 us (33%)
  local copies, waits for them, and re-layouts  96.7 us (11%)
  other arithmetic  21.9 us (3%)
  between operations  14.4 us (2%)
  starting transfers between devices  13 us (2%)
    pallas_call x10, Pallas kernels, heads_call(): pl.pallas_call(functools.partial(heads_kernel, n_heads, seq_len, o_in is...  204 us
    all_gather x3, waiting for transfers between devices, gather_shards(): mine_all = lax.all_gather(mine, 't', axis=0, tiled=False)  153 us
    ppermute x2, waiting for transfers between devices, on_cache_side(): back = lax.ppermute(y_s, 'stage', back_pairs)  124 us
    ppermute x2, waiting for transfers between devices, for_both(): return (y_s, lax.ppermute(y_s, 't', [(t, t ^ 1) for t in range(n_tp)]))  97.1 us
    pallas_call x5, Pallas kernels, out_call(): pl.pallas_call(functools.partial(out_kernel, d_model), out_shape=jax.Shap...  62.5 us
    ppermute x1, waiting for transfers between devices, layer(): lax.ppermute(lax.dynamic_slice_in_dim(tokens, t_index * n_away, 1, axis=0...  52.9 us
    dynamic_update_slice x6, local copies, waits for them, and re-layouts, layer(): rows = lax.dynamic_update_slice_in_dim(rows, piece, place, axis=0)  34 us
    unnamed x54, local copies, waits for them, and re-layouts  29.7 us
  transfers between devices with their start and end apart: 12, of which 5 were waited for; matrix products, arithmetic and copies ran while one was open for 11% of the time, Pallas kernels for 31%

profile of v2, /device:TPU:12, one launch (start us, length us, event | category | flops | bytes accessed | tf_op | source)
XLA Modules:
  0.0 861.6 jit_solution(4229791025096783388)
XLA Ops:
  10.6 4.6 copy.17
  28.9 12.0 %dynamic-slice_bitcast_fusion = (bf16[1,1536,2048]{2,1,0:T(8,128)(2,1)}, bf16[1,1536,2048]{2,1,0:T(8,128)(2,1)}) fusion(bf16[1,8,1536,2048]{3,2,1,0:T(8,128)(2,1)} %param.7, s32[]{:T(128)S(6)} %select_n.95, s32[]{:T(128)S(6)} %select_n.92), kind=kLoop, calls=%fused_computation.6 | loop fusion | bytes 25165832 | tf_op jit(solution)/shard_map/dynamic_slice | solution.py:292
  49.8 4.3 copy.16
  65.3 8.1 shard_map.87.refs_9_
  73.4 7.5 shard_map.93.refs_9_
  85.0 86.1 %all-gather.7.cloned.1.call-done = bf16[4096,768]{1,0:T(8,128)(2,1)} async-done(((bf16[1024,768]{1,0:T(8,128)(2,1)}), bf16[4096,768]{1,0:T(8,128)(2,1)}) %all-gather.7.cloned.1.call-update) | async-done | bytes 6291472 | tf_op jit(solution)/shard_map/all_gather | solution.py:270
  172.6 7.1 shard_map.90.refs_9_
  185.0 66.9 %all-gather.11.cloned.1.call-done = bf16[1024,2048]{1,0:T(8,128)(2,1)} async-done(((bf16[256,2048]{1,0:T(8,128)(2,1)}), bf16[1024,2048]{1,0:T(8,128)(2,1)}) %all-gather.11.cloned.1.call-update) | async-done | bytes 4194320 | tf_op jit(solution)/shard_map/all_gather | solution.py:270
  251.9 9.4 %shard_map.100 = (bf16[1,1536,512]{2,1,0:T(8,128)(2,1)S(1)}, bf16[1,1536,256]{2,1,0:T(8,128)(2,1)S(1)}) custom-call(s32[2]{0:T(128)S(1)} %pad_add_fusion.8.meta, bf16[1,1536,2048]{2,1,0:T(8,128)(2,1)} %collective-permute-done.7.x_ref.refs_1_, bf16[2048,640]{1,0:T(8,128)(2,1)} %copy-done.6, f32[1,512]{1,0:T(1,128)S(1)} %bitcast.44, ...), custom_call_target="tpu_custom_call" | custom-call | flops 4026531840 | bytes 6291456 | tf_op jit(solution)/shard_map/pallas_call | solution.py:71
  262.2 52.9 %collective-permute-done.3.x_ref.refs_1_ = bf16[1,1536,2048]{2,1,0:T(8,128)(2,1)} collective-permute-done((bf16[1,1536,2048]{2,1,0:T(8,128)(2,1)}, bf16[1,1536,2048]{2,1,0:T(8,128)(2,1)}, u32[]{:S(2)}, u32[]{:S(2)}) %collective-permute-start.3) | collective-permute-done | bytes 6291488 | tf_op jit(solution)/shard_map/ppermute | solution.py:291
  315.1 9.4 %shard_map.96 = (bf16[1,1536,512]{2,1,0:T(8,128)(2,1)S(1)}, bf16[1,1536,256]{2,1,0:T(8,128)(2,1)S(1)}) custom-call(s32[2]{0:T(128)S(1)} %pad_add_fusion.8.meta, bf16[1,1536,2048]{2,1,0:T(8,128)(2,1)} %collective-permute-done.3.x_ref.refs_1_, bf16[2048,640]{1,0:T(8,128)(2,1)} %copy-done.6, f32[1,512]{1,0:T(1,128)S(1)} %bitcast.45, f32[1536,128]{1,0:T(8,128)S(1)} %copy-done.3, ...), custom_call_target="tpu_custom_call" | custom-call | flops 4026531840 | bytes 6291456 | tf_op jit(solution)/shard_map/pallas_call | solution.py:71
  328.6 6.1 copy.20
  334.8 23.1 %shard_map.101.refs_9_ = bf16[1,1536,2048]{2,1,0:T(8,128)(2,1)} custom-call(s32[5]{0:T(128)} %get-tuple-element.22.refs_0_, bf16[1,1536,2048]{2,1,0:T(8,128)(2,1)} %collective-permute-done.7.x_ref.refs_1_, bf16[1,1536,512]{2,1,0:T(8,128)(2,1)} %copy-done.8, bf16[1,1536,256]{2,1,0:T(8,128)(2,1)} %copy-done.10, bf16[1,2048,768]{2,1,0:T(8,128)(2,1)} %fusion.refs_4_.refs_5_, ...), custom_call_target="tpu_custom_call" | custom-call | flops 12079595520 | bytes 6291456 | tf_op jit(solution)/shard_map/pallas_call | solution.py:235
  357.9 23.8 %shard_map.97.refs_9_ = bf16[1,1536,2048]{2,1,0:T(8,128)(2,1)} custom-call(s32[5]{0:T(128)} %get-tuple-element.22.refs_0_, bf16[1,1536,2048]{2,1,0:T(8,128)(2,1)} %collective-permute-done.3.x_ref.refs_1_, bf16[1,1536,512]{2,1,0:T(8,128)(2,1)} %copy-done.7, bf16[1,1536,256]{2,1,0:T(8,128)(2,1)} %copy-done.9, bf16[1,2048,768]{2,1,0:T(8,128)(2,1)} %fusion.refs_4_.refs_5_, ...), custom_call_target="tpu_custom_call" | custom-call | flops 12079595520 | bytes 6291456 | tf_op jit(solution)/shard_map/pallas_call | solution.py:235
  381.7 56.1 %shard_map.102.o_ref = bf16[1,1536,2048]{2,1,0:T(8,128)(2,1)} custom-call(s32[9]{0:T(128)} %concatenate.100.refs_0_, bf16[1,1536,2048]{2,1,0:T(8,128)(2,1)} %collective-permute-done.7.x_ref.refs_1_, bf16[1,1536,512]{2,1,0:T(8,128)(2,1)} %copy-done.8, bf16[1,1536,256]{2,1,0:T(8,128)(2,1)} %copy-done.10, ...), custom_call_target="tpu_custom_call", output_to_operand_aliasing={{}: (9, {})} | custom-call | flops 36238786560 | bytes 18874368 | tf_op jit(solution)/shard_map/pallas_call | solution.py:235
  440.0 20.5 %shard_map.103 = bf16[1,1536,2048]{2,1,0:T(8,128)(2,1)} custom-call(s32[3]{0:T(128)S(1)} %pad_add_fusion.meta, bf16[1,1536,2048]{2,1,0:T(8,128)(2,1)} %shard_map.102.o_ref, bf16[4,256,2048]{2,1,0:T(8,128)(2,1)S(1)} %bitcast.47, bf16[4,256,2048]{2,1,0:T(8,128)(2,1)} %collective-permute-done.2.twin_ref), custom_call_target="tpu_custom_call" | custom-call | flops 12884901888 | bytes 12582912 | tf_op jit(solution)/shard_map/pallas_call | solution.py:114
  464.4 56.4 %shard_map.98.o_ref = bf16[1,1536,2048]{2,1,0:T(8,128)(2,1)} custom-call(s32[9]{0:T(128)} %concatenate.100.refs_0_, bf16[1,1536,2048]{2,1,0:T(8,128)(2,1)} %collective-permute-done.3.x_ref.refs_1_, bf16[1,1536,512]{2,1,0:T(8,128)(2,1)} %copy-done.7, bf16[1,1536,256]{2,1,0:T(8,128)(2,1)} %copy-done.9, ...), custom_call_target="tpu_custom_call", output_to_operand_aliasing={{}: (9, {})} | custom-call | flops 36238786560 | bytes 18874368 | tf_op jit(solution)/shard_map/pallas_call | solution.py:235
  523.0 20.5 %shard_map.99 = bf16[1,1536,2048]{2,1,0:T(8,128)(2,1)} custom-call(s32[3]{0:T(128)S(1)} %pad_add_fusion.meta, bf16[1,1536,2048]{2,1,0:T(8,128)(2,1)} %shard_map.98.o_ref, bf16[4,256,2048]{2,1,0:T(8,128)(2,1)S(1)} %bitcast.48, bf16[4,256,2048]{2,1,0:T(8,128)(2,1)} %collective-permute-done.2.twin_ref), custom_call_target="tpu_custom_call" | custom-call | flops 12884901888 | bytes 12582912 | tf_op jit(solution)/shard_map/pallas_call | solution.py:114
  543.5 4.1 collective-permute-start.4
  547.6 7.1 shard_map.94.o_ref
  556.9 6.4 shard_map.95
  563.6 7.1 shard_map.91.o_ref
  572.9 6.3 shard_map.92
  580.9 7.4 shard_map.88.o_ref
  590.5 8.7 %shard_map.89 = bf16[8,1536,2048]{2,1,0:T(8,128)(2,1)} custom-call(s32[4]{0:T(128)S(1)} %add_add_fusion.meta, bf16[4,1536,2048]{2,1,0:T(8,128)(2,1)} %shard_map.88.o_ref, bf16[4,256,2048]{2,1,0:T(8,128)(2,1)S(1)} %bitcast.51, bf16[4,256,2048]{2,1,0:T(8,128)(2,1)} %collective-permute-done.2.twin_ref), custom_call_target="tpu_custom_call" | custom-call | flops 25769803776 | bytes 25165824 | tf_op jit(solution)/shard_map/pallas_call | solution.py:114
  599.2 4.1 bitcast_dynamic-update-slice_fusion.5
  607.1 124.0 %collective-permute-done.4 = bf16[1,1536,2048]{2,1,0:T(8,128)(2,1)} collective-permute-done((bf16[1,1536,2048]{2,1,0:T(8,128)(2,1)}, bf16[1,1536,2048]{2,1,0:T(8,128)(2,1)}, u32[]{:S(2)}, u32[]{:S(2)}) %collective-permute-start.4) | collective-permute-done | bytes 6291488 | tf_op jit(solution)/shard_map/ppermute | solution.py:339
  731.1 6.6 bitcast_dynamic-update-slice_fusion.3
  737.8 97.1 %collective-permute-done.5 = bf16[1,1536,2048]{2,1,0:T(8,128)(2,1)} collective-permute-done((bf16[1,1536,2048]{2,1,0:T(8,128)(2,1)}, bf16[1,1536,2048]{2,1,0:T(8,128)(2,1)}, u32[]{:S(2)}, u32[]{:S(2)}) %collective-permute-start.5) | collective-permute-done | bytes 6291488 | tf_op jit(solution)/shard_map/ppermute | solution.py:347
  834.9 6.6 bitcast_dynamic-update-slice_fusion.2
  841.5 6.8 bitcast_dynamic-update-slice_fusion.1
  848.2 6.6 bitcast_dynamic-update-slice_fusion
  (115 shorter events, 73.4 us)
Async XLA Ops:
  7.2 36.6 %copy-start = (bf16[512,2048]{1,0:T(8,128)(2,1)S(1)}, bf16[512,2048]{1,0:T(8,128)(2,1)}, u32[]{:S(2)}) copy-start(bf16[512,2048]{1,0:T(8,128)(2,1)} %param.13) | copy-start | bytes 6291460
  7.2 66.2 %all-gather.9.cloned.1.call-start = ((), (), s32[]{:S(2)}) async-start(), calls=%async_computation.1 | async-start | bytes 2621440 | tf_op jit(solution)/shard_map/all_gather | solution.py:270
  9.6 7.9 copy-start.17
  10.6 160.5 %all-gather.7.cloned.1.call-start = ((), (), s32[]{:S(2)}) async-start(), calls=%async_computation | async-start | bytes 7864320 | tf_op jit(solution)/shard_map/all_gather | solution.py:270
  28.8 223.1 %all-gather.11.cloned.1.call-start = ((), (), s32[]{:S(2)}) async-start(), calls=%async_computation.2 | async-start | bytes 5242880 | tf_op jit(solution)/shard_map/all_gather | solution.py:270
  28.8 17.0 %copy-start.22 = (bf16[512]{0:T(512)(128)(2,1)S(1)}, bf16[512]{0:T(512)(128)(2,1)}, u32[]{:S(2)}) copy-start(bf16[512]{0:T(512)(128)(2,1)} %param.10) | copy-start | bytes 3076
  40.8 211.0 %collective-permute-start.7 = (bf16[1,1536,2048]{2,1,0:T(8,128)(2,1)}, bf16[1,1536,2048]{2,1,0:T(8,128)(2,1)}, u32[]{:S(2)}, u32[]{:S(2)}) collective-permute-start(bf16[1,1536,2048]{2,1,0:T(8,128)(2,1)} %get-tuple-element.18), channel_id=1, source_target_pairs={{0,2},{1,3},{4,6},{5,7},{8,10},{9,11},{12,14},{13,15},{16,18},{17,... | collective-permute-start | bytes 18874376 | tf_op jit(solution)/shard_map/ppermute | solution.py:292
  42.1 273.0 %collective-permute-start.3 = (bf16[1,1536,2048]{2,1,0:T(8,128)(2,1)}, bf16[1,1536,2048]{2,1,0:T(8,128)(2,1)}, u32[]{:S(2)}, u32[]{:S(2)}) collective-permute-start(bf16[1,1536,2048]{2,1,0:T(8,128)(2,1)} %get-tuple-element.19), channel_id=1, source_target_pairs={{0,2},{1,3},{4,6},{5,7},{8,10},{9,11},{12,14},{13,15},{16,18},{17,... | collective-permute-start | bytes 18874376 | tf_op jit(solution)/shard_map/ppermute | solution.py:291
  54.1 4.2 copy-start.19
  54.1 4.2 copy-start.20
  54.1 4.2 copy-start.21
  56.2 7.1 copy-start.6
  59.6 3.7 copy-start.2
  59.6 3.7 copy-start.4
  59.6 3.7 copy-start.16
  73.4 106.2 %collective-permute-start.1 = (bf16[4,256,1024]{2,1,0:T(8,128)(2,1)}, bf16[4,256,1024]{2,1,0:T(8,128)(2,1)}, u32[]{:S(2)}, u32[]{:S(2)}) collective-permute-start(bf16[4,256,1024]{2,1,0:T(8,128)(2,1)} %bitcast.70), channel_id=1, source_target_pairs={{0,1},{1,0},{2,3},{3,2},{4,5},{5,4},{6,7},{7,6},{8,9},{9,8},{10,11... | collective-permute-start | bytes 6291464 | tf_op jit(solution)/shard_map/ppermute | solution.py:271
  171.1 210.6 %collective-permute-start = (bf16[4,1024,768]{2,1,0:T(8,128)(2,1)}, bf16[4,1024,768]{2,1,0:T(8,128)(2,1)}, u32[]{:S(2)}, u32[]{:S(2)}) collective-permute-start(bf16[4,1024,768]{2,1,0:T(8,128)(2,1)} %bitcast.75), channel_id=1, source_target_pairs={{0,1},{1,0},{2,3},{3,2},{4,5},{5,4},{6,7},{7,6},{8,9},{9,8},{10,11... | collective-permute-start | bytes 18874376 | tf_op jit(solution)/shard_map/ppermute | solution.py:271
  182.5 69.4 %copy-start.3 = (f32[1536,128]{1,0:T(8,128)S(1)}, f32[1536,128]{1,0:T(8,128)}, u32[]{:S(2)}) copy-start(f32[1536,128]{1,0:T(8,128)} %copy-done.2) | copy-start | bytes 2359300
  182.5 69.4 %copy-start.5 = (f32[1536,128]{1,0:T(8,128)S(1)}, f32[1536,128]{1,0:T(8,128)}, u32[]{:S(2)}) copy-start(f32[1536,128]{1,0:T(8,128)} %copy-done.4) | copy-start | bytes 2359300
  251.9 186.0 %collective-permute-start.2 = (bf16[4,256,2048]{2,1,0:T(8,128)(2,1)}, bf16[4,256,2048]{2,1,0:T(8,128)(2,1)}, u32[]{:S(2)}, u32[]{:S(2)}) collective-permute-start(bf16[4,256,2048]{2,1,0:T(8,128)(2,1)} %bitcast.46), channel_id=1, source_target_pairs={{0,1},{1,0},{2,3},{3,2},{4,5},{5,4},{6,7},{7,6},{8,9},{9,8},{10,11... | collective-permute-start | bytes 12582920 | tf_op jit(solution)/shard_map/ppermute | solution.py:271
  261.4 63.3 %copy-start.8 = (bf16[1,1536,512]{2,1,0:T(8,128)(2,1)}, bf16[1,1536,512]{2,1,0:T(8,128)(2,1)S(1)}, u32[]{:S(2)}) copy-start(bf16[1,1536,512]{2,1,0:T(8,128)(2,1)S(1)} %get-tuple-element.12.refs_2_) | copy-start | bytes 4718596
  437.8 2.2 copy-start.11
  460.5 387.7 %collective-permute-start.8 = (bf16[1,1536,2048]{2,1,0:T(8,128)(2,1)}, bf16[1,1536,2048]{2,1,0:T(8,128)(2,1)}, u32[]{:S(2)}, u32[]{:S(2)}) collective-permute-start(bf16[1,1536,2048]{2,1,0:T(8,128)(2,1)} %shard_map.103), channel_id=1, source_target_pairs={{2,0},{3,1},{6,4},{7,5},{10,8},{11,9},{14,12},{15,13},{18,16},{19,... | collective-permute-start | bytes 18874376 | tf_op jit(solution)/shard_map/ppermute | solution.py:339
  543.5 187.6 %collective-permute-start.4 = (bf16[1,1536,2048]{2,1,0:T(8,128)(2,1)}, bf16[1,1536,2048]{2,1,0:T(8,128)(2,1)}, u32[]{:S(2)}, u32[]{:S(2)}) collective-permute-start(bf16[1,1536,2048]{2,1,0:T(8,128)(2,1)} %shard_map.99), channel_id=1, source_target_pairs={{2,0},{3,1},{6,4},{7,5},{10,8},{11,9},{14,12},{15,13},{18,16},{19,... | collective-permute-start | bytes 18874376 | tf_op jit(solution)/shard_map/ppermute | solution.py:339
  554.7 2.2 copy-start.13
  563.3 278.2 %collective-permute-start.6 = (bf16[1,1536,2048]{2,1,0:T(8,128)(2,1)}, bf16[1,1536,2048]{2,1,0:T(8,128)(2,1)}, u32[]{:S(2)}, u32[]{:S(2)}) collective-permute-start(bf16[1,1536,2048]{2,1,0:T(8,128)(2,1)} %shard_map.95), channel_id=1, source_target_pairs={{0,4},{4,0},{8,12},{12,8},{1,5},{5,1},{9,13},{13,9},{2,6},{6,2},{1... | collective-permute-start | bytes 18874376 | tf_op jit(solution)/shard_map/ppermute | solution.py:347
  570.7 2.2 copy-start.14
  579.2 255.6 %collective-permute-start.5 = (bf16[1,1536,2048]{2,1,0:T(8,128)(2,1)}, bf16[1,1536,2048]{2,1,0:T(8,128)(2,1)}, u32[]{:S(2)}, u32[]{:S(2)}) collective-permute-start(bf16[1,1536,2048]{2,1,0:T(8,128)(2,1)} %shard_map.92), channel_id=1, source_target_pairs={{0,4},{4,0},{8,12},{12,8},{1,5},{5,1},{9,13},{13,9},{2,6},{6,2},{1... | collective-permute-start | bytes 18874376 | tf_op jit(solution)/shard_map/ppermute | solution.py:347
  590.5 8.7 %copy-start.18 = (bf16[1,1536,2048]{2,1,0:T(8,128)(2,1)S(1)}, bf16[1,1536,2048]{2,1,0:T(8,128)(2,1)}, u32[]{:S(2)}) copy-start(bf16[1,1536,2048]{2,1,0:T(8,128)(2,1)} %shard_map.92) | copy-start | bytes 18874372
  599.2 4.1 slice-start
  599.2 4.6 slice-start.1
  841.5 13.4 %copy-start.1 = (bf16[512,2048]{1,0:T(8,128)(2,1)S(1)}, bf16[512,2048]{1,0:T(8,128)(2,1)}, u32[]{:S(2)}) copy-start(bf16[512,2048]{1,0:T(8,128)(2,1)} %param.13) | copy-start | bytes 6291460
  (5 other events, 7.8 us)
Sparse Core Ops, SparseCore 0:
  10.7 45.4 all-gather.8
  58.3 112.6 all-gather.6
  172.6 79.2 all-gather.10
